TPU v7x, 256 devices: a whole 4x4x8 slice. The times are simulated.
256 devices in a mesh: patch: 128 (over x, y, z), col: 2 (over core).
Axes of the slice: x: 4, y: 4, z: 8, core: 2. Of those that a mesh axis runs over, the one named last changes fastest.
Arguments:
- density: float32 [4, 131072], P(None, 'patch'), may hold values from -6 to 6
- block_values: bfloat16 [512, 32, 256, 256], P('patch', 'col'), may hold values from -0.09375 to 0.09375
- block_rows: int32 [512, 32], P('patch', 'col'), may hold values from 0 to 511, as said below
- block_counts: int32 [512], P('patch'), may hold values from 1 to 32
Outputs:
- potential: float32 [4, 131072], P(None, 'patch')
Inputs may be any that keep to these rules, and one draw needn't show every extreme that they name: `block_rows`: slots of a block column at or past its count are padding and are not part of the matrix. Block row r belongs to owner r // 4. The slots held by one device (block columns of one patch owner, one col index, live or padding) name block rows of distinct owners in groups of exactly 2 slots a group, so at most 2 of them fall on one owner.
All inputs are finite; a program needn't handle non-finite values.
Results may differ from a plain program's by a relative error of at most 0.0027.
Values sent between devices are 32-bit elements; how exact they have to be, the bound alone decides.
No kernel may reach another device: no remote copies, remote signals or barrier semaphores. Data moves between devices by JAX's collectives and lax.ppermute only.
A program may use at most 64 MiB of HBM per device.

v0:
```python
import jax
import jax.numpy as jnp
from jax import lax
from jax.sharding import PartitionSpec as P

LEVELS = 3


def with_halo(block, sides, width):
    for axis, dim in sides:
        count = lax.axis_size(axis)
        forward = [(i, i + 1) for i in range(count - 1)]
        backward = [(target, source) for source, target in forward]
        low = lax.ppermute(
            lax.slice_in_dim(block, block.shape[dim] - width, None, axis=dim), axis, forward
        )
        high = lax.ppermute(lax.slice_in_dim(block, 0, width, axis=dim), axis, backward)
        block = jnp.concatenate([low, block, high], axis=dim)
    return block


def total_of_pieces(array, axis):
    parts = lax.all_gather(array, axis)
    return parts.sum(axis=0)


def inside_mask(length, margin):
    where = (
        lax.axis_index("patch") * length + jnp.arange(length + 2 * margin, dtype=jnp.int32) - margin
    )
    valid = (where >= 0) & (where < lax.axis_size("patch") * length)
    return valid.astype(jnp.float32)[None, :]


def body(density, block_values, block_rows, block_counts):
    sides = density.shape[0]
    col_blocks = block_values.shape[0]
    slots = block_values.shape[1]
    block = block_values.shape[2]
    local_len = density.shape[1]
    details = []
    reach = 2 ** (LEVELS + 1)
    smooth = with_halo(density, (("patch", 1),), reach)
    for level_index in range(LEVELS):
        margin = reach // 2 ** (level_index + 1)
        length = local_len // 2 ** (level_index + 1)
        keep = inside_mask(length, margin)
        even_part = smooth[:, 0::2]
        odd_part = smooth[:, 1::2]
        zero_col = jnp.zeros_like(even_part[:, :1])
        even_next = jnp.concatenate([even_part[:, 1:], zero_col], axis=1)
        detail = (odd_part - 0.5 * (even_part + even_next)) * keep
        detail_prior = jnp.concatenate([zero_col, detail[:, :-1]], axis=1)
        smooth = (even_part + 0.25 * (detail_prior + detail)) * keep
        details.append(detail[:, margin : margin + length])
    smooth = smooth[:, margin : margin + length]
    vector = jnp.concatenate([smooth] + details[::-1], axis=1).astype(jnp.bfloat16)
    blocks = vector.reshape(sides, col_blocks, block).transpose(1, 0, 2)
    terms = jnp.einsum("cjkm,crm->cjrk", block_values, blocks, preferred_element_type=jnp.float32)
    first_slot = lax.axis_index("col") * slots
    live = first_slot + jnp.arange(slots, dtype=jnp.int32)[None, :] < block_counts[:, None]
    owners = lax.axis_size("patch")
    width = sides * block
    held = col_blocks * slots
    capacity = max(2, (2 * held + owners - 1) // owners)
    flat_terms = terms.reshape(held, width) * live.reshape(held, 1).astype(jnp.float32)
    flat_rows = block_rows.reshape(held)
    target = flat_rows // col_blocks
    inside = flat_rows % col_blocks
    order_ids = jnp.arange(held, dtype=jnp.int32)
    earlier = (target[:, None] == target[None, :]) & (order_ids[:, None] > order_ids[None, :])
    rank = jnp.sum(earlier.astype(jnp.int32), axis=1)
    place = (target * capacity + rank)[None, :] == jnp.arange(owners * capacity, dtype=jnp.int32)[
        :, None
    ]
    outgoing = jnp.dot(place.astype(jnp.float32), flat_terms, precision=lax.Precision.HIGHEST)
    row_ids = jnp.sum(jnp.where(place, inside[None, :], 0), axis=1)
    arrived, arrived_ids = (
        lax.all_to_all(
            outgoing.reshape(owners, capacity, width),
            "patch",
            split_axis=0,
            concat_axis=0,
            tiled=True,
        ),
        lax.all_to_all(
            row_ids.reshape(owners, capacity), "patch", split_axis=0, concat_axis=0, tiled=True
        ),
    )
    landing = arrived_ids.reshape(1, -1) == jnp.arange(col_blocks, dtype=jnp.int32)[:, None]
    mine = jnp.dot(
        landing.astype(jnp.float32), arrived.reshape(-1, width), precision=lax.Precision.HIGHEST
    )
    summed = total_of_pieces(mine, "col")
    local = summed.reshape(col_blocks, sides, block).transpose(1, 0, 2).reshape(sides, local_len)
    coarse = local_len // 2**LEVELS
    bounds = [(0, coarse)]
    for level_index in range(LEVELS, 0, -1):
        bounds.append((local_len // 2**level_index, local_len // 2 ** (level_index - 1)))
    pieces = [local[:, lower:upper] for lower, upper in bounds]
    edges = jnp.stack(
        [jnp.concatenate([piece[:, :2], piece[:, -2:]], axis=1) for piece in pieces], axis=1
    )
    widened = with_halo(edges, (("patch", 2),), 2)
    extended = [
        jnp.concatenate([widened[:, index, :2], piece, widened[:, index, 6:8]], axis=1)
        for index, piece in enumerate(pieces)
    ]
    smooth = extended[0]
    for step_index in range(LEVELS):
        detail = extended[step_index + 1]
        length = detail.shape[1] - 4
        keep = inside_mask(length, 2)
        zero_col = jnp.zeros_like(detail[:, :1])
        detail_prior = jnp.concatenate([zero_col, detail[:, :-1]], axis=1)
        even_part = (smooth - 0.25 * (detail_prior + detail)) * keep
        even_next = jnp.concatenate([even_part[:, 1:], zero_col], axis=1)
        odd_part = detail + 0.5 * (even_part + even_next)
        smooth = jnp.stack([even_part, odd_part], axis=-1).reshape(sides, -1)[:, 2:-2]
    smooth = smooth[:, 2:-2]
    return 0.5 * density + smooth


def solution(mesh):
    return jax.shard_map(
        body,
        mesh=mesh,
        in_specs=(P(None, "patch"), P("patch", "col", None, None), P("patch", "col"), P("patch")),
        out_specs=P(None, "patch"),
        check_vma=False,
    )
```

profile of v0, /device:TPU:6, one launch (start us, length us, event | category | flops | bytes accessed | tf_op | source)
XLA Modules:
  0.0 98.0 jit_solution(15631667738479460056)
XLA Ops:
  0.0 0.8 fusion.29
  0.8 3.8 %collective-permute-start = (f32[4,16]{1,0:T(4,128)S(1)}, f32[4,16]{1,0:T(4,128)S(1)}, u32[]{:S(2)}, u32[]{:S(2)}) collective-permute-start(f32[4,16]{1,0:T(4,128)S(1)} %get-tuple-element.16), channel_id=1, source_target_pairs={{0,2},{2,4},{4,6},{6,8},{8,10},{10,12},{12,14},{14,16},{16,18},{18... | collective-permute-start | bytes 776 | tf_op jit(solution)/shard_map/ppermute | solution.py:14
  4.6 8.6 %collective-permute-start.1 = (f32[4,16]{1,0:T(4,128)S(1)}, f32[4,16]{1,0:T(4,128)S(1)}, u32[]{:S(2)}, u32[]{:S(2)}) collective-permute-start(f32[4,16]{1,0:T(4,128)S(1)} %get-tuple-element.15), channel_id=1, source_target_pairs={{2,0},{4,2},{6,4},{8,6},{10,8},{12,10},{14,12},{16,14},{18,16},{20... | collective-permute-start | bytes 776 | tf_op jit(solution)/shard_map/ppermute | solution.py:17
  13.2 0.8 reshape.211
  14.0 0.2 convert_reduce_fusion
  14.2 0.8 all_to_all.9
  15.0 10.6 %all-to-all-start = ((s32[128,1,2]{2,1,0:T(1,128)}), s32[128,1,2]{2,1,0:T(1,128)S(1)}, u32[]{:S(2)}, u32[]{:S(2)}) async-start(s32[128,1,2]{2,1,0:T(1,128)} %bitcast), calls=%async_computation | async-start | bytes 131072 | tf_op jit(solution)/shard_map/all_to_all | solution.py:86
  25.6 0.7 compare_convert_fusion
  26.5 0.8 concatenate.67
  27.3 0.4 slice.163
  27.7 0.4 slice.164
  28.2 0.2 slice.167
  28.4 0.2 slice.168
  28.9 0.2 slice.171
  29.1 0.2 slice.172
  29.7 5.6 %fusion = f32[4,16,4,256]{3,2,1,0:T(4,128)S(1)} fusion(bf16[4,4,256,1]{2,1,3,0:T(4,128)(2,1)S(1)} %bitcast.74, bf16[4,16,256,256]{3,2,1,0:T(8,128)(2,1)} %param.5, f32[4,16]{1,0:T(4,128)S(1)} %compare_convert_fusion), kind=kOutput, calls=%fused_computation.1 | convolution fusion | flops 33619968 | bytes 8659200 | tf_op jit(solution)/shard_map/cjkm,crm->cjrk/dot_general | solution.py:59
  35.5 0.7 fusion.1
  36.2 1.8 %copy.151 = f32[128,2,1024]{2,1,0:T(2,128)} copy(f32[128,2,1024]{2,0,1:T(8,128)S(1)} %fusion.1) | data formatting | bytes 2097152 | tf_op jit(solution)/shard_map/dot_general | solution.py:76
  38.0 13.8 %all-to-all-start.1 = ((f32[128,2,1024]{2,1,0:T(2,128)}), f32[128,2,1024]{2,1,0:T(2,128)S(1)}, u32[]{:S(2)}, u32[]{:S(2)}) async-start(f32[128,2,1024]{2,1,0:T(2,128)} %copy.151), calls=%async_computation.1 | async-start | bytes 2097152 | tf_op jit(solution)/shard_map/all_to_all | solution.py:79
  51.9 0.5 broadcast.304
  52.4 0.8 reduce.4
  53.3 27.1 %all-to-all-done.1 = f32[128,2,1024]{2,1,0:T(2,128)S(1)} async-done(((f32[128,2,1024]{2,1,0:T(2,128)}), f32[128,2,1024]{2,1,0:T(2,128)S(1)}, u32[]{:S(2)}, u32[]{:S(2)}) %all-to-all-start.1) | async-done | bytes 1048608 | tf_op jit(solution)/shard_map/all_to_all | solution.py:79
  80.4 0.7 reshape.212
  81.1 0.4 convolution_bitcast_fusion
  81.6 1.8 %all-gather.1 = f32[2,4,1024]{2,1,0:T(4,128)S(1)} all-gather(f32[1,4,1024]{2,1,0:T(4,128)S(1)} %convolution_bitcast_fusion), channel_id=2, replica_groups=mesh['patch'=128,'col'=2] {'col'}, dimensions={0}, use_global_device_ids=true | all-gather | bytes 49152 | tf_op jit(solution)/shard_map/all_gather | solution.py:23
  83.7 2.5 %collective-permute-start.2 = (f32[4,4,2]{2,0,1:T(4,128)S(1)}, f32[4,4,2]{2,0,1:T(4,128)S(1)}, u32[]{:S(2)}, u32[]{:S(2)}) collective-permute-start(f32[4,4,2]{2,0,1:T(4,128)S(1)} %get-tuple-element.25), channel_id=1, source_target_pairs={{0,2},{2,4},{4,6},{6,8},{8,10},{10,12},{12,14},{14,16},{16,18},{18... | collective-permute-start | bytes 392 | tf_op jit(solution)/shard_map/ppermute | solution.py:14
  86.2 7.6 %collective-permute-start.3 = (f32[4,4,2]{2,0,1:T(4,128)S(1)}, f32[4,4,2]{2,0,1:T(4,128)S(1)}, u32[]{:S(2)}, u32[]{:S(2)}) collective-permute-start(f32[4,4,2]{2,0,1:T(4,128)S(1)} %get-tuple-element.26), channel_id=1, source_target_pairs={{2,0},{4,2},{6,4},{8,6},{10,8},{12,10},{14,12},{16,14},{18,16},{20... | collective-permute-start | bytes 392 | tf_op jit(solution)/shard_map/ppermute | solution.py:17
  93.8 1.3 %collective-permute-done.3 = f32[4,4,2]{2,0,1:T(4,128)S(1)} collective-permute-done((f32[4,4,2]{2,0,1:T(4,128)S(1)}, f32[4,4,2]{2,0,1:T(4,128)S(1)}, u32[]{:S(2)}, u32[]{:S(2)}) %collective-permute-start.3) | collective-permute-done | bytes 160 | tf_op jit(solution)/shard_map/ppermute | solution.py:17
  96.1 0.2 copy.166
  96.9 0.3 copy.172
  97.2 0.2 copy.185
  97.4 0.6 multiply_add_fusion
  (65 shorter events, 3.1 us)
Async XLA Ops:
  0.8 25.7 %collective-permute-start = (f32[4,16]{1,0:T(4,128)S(1)}, f32[4,16]{1,0:T(4,128)S(1)}, u32[]{:S(2)}, u32[]{:S(2)}) collective-permute-start(f32[4,16]{1,0:T(4,128)S(1)} %get-tuple-element.16), channel_id=1, source_target_pairs={{0,2},{2,4},{4,6},{6,8},{8,10},{10,12},{12,14},{14,16},{16,18},{18... | collective-permute-start | bytes 776 | tf_op jit(solution)/shard_map/ppermute | solution.py:14
  4.6 21.9 %collective-permute-start.1 = (f32[4,16]{1,0:T(4,128)S(1)}, f32[4,16]{1,0:T(4,128)S(1)}, u32[]{:S(2)}, u32[]{:S(2)}) collective-permute-start(f32[4,16]{1,0:T(4,128)S(1)} %get-tuple-element.15), channel_id=1, source_target_pairs={{2,0},{4,2},{6,4},{8,6},{10,8},{12,10},{14,12},{16,14},{18,16},{20... | collective-permute-start | bytes 776 | tf_op jit(solution)/shard_map/ppermute | solution.py:17
  15.0 23.0 %all-to-all-start = ((s32[128,1,2]{2,1,0:T(1,128)}), s32[128,1,2]{2,1,0:T(1,128)S(1)}, u32[]{:S(2)}, u32[]{:S(2)}) async-start(s32[128,1,2]{2,1,0:T(1,128)} %bitcast), calls=%async_computation | async-start | bytes 131072 | tf_op jit(solution)/shard_map/all_to_all | solution.py:86
  35.4 62.0 %copy-start = (f32[4,1024]{1,0:T(4,128)S(1)}, f32[4,1024]{1,0:T(4,128)}, u32[]{:S(2)}) copy-start(f32[4,1024]{1,0:T(4,128)} %param.4) | copy-start | bytes 49156
  38.0 42.4 %all-to-all-start.1 = ((f32[128,2,1024]{2,1,0:T(2,128)}), f32[128,2,1024]{2,1,0:T(2,128)S(1)}, u32[]{:S(2)}, u32[]{:S(2)}) async-start(f32[128,2,1024]{2,1,0:T(2,128)} %copy.151), calls=%async_computation.1 | async-start | bytes 2097152 | tf_op jit(solution)/shard_map/all_to_all | solution.py:79
  83.7 10.1 %collective-permute-start.2 = (f32[4,4,2]{2,0,1:T(4,128)S(1)}, f32[4,4,2]{2,0,1:T(4,128)S(1)}, u32[]{:S(2)}, u32[]{:S(2)}) collective-permute-start(f32[4,4,2]{2,0,1:T(4,128)S(1)} %get-tuple-element.25), channel_id=1, source_target_pairs={{0,2},{2,4},{4,6},{6,8},{8,10},{10,12},{12,14},{14,16},{16,18},{18... | collective-permute-start | bytes 392 | tf_op jit(solution)/shard_map/ppermute | solution.py:14
  86.2 8.9 %collective-permute-start.3 = (f32[4,4,2]{2,0,1:T(4,128)S(1)}, f32[4,4,2]{2,0,1:T(4,128)S(1)}, u32[]{:S(2)}, u32[]{:S(2)}) collective-permute-start(f32[4,4,2]{2,0,1:T(4,128)S(1)} %get-tuple-element.26), channel_id=1, source_target_pairs={{2,0},{4,2},{6,4},{8,6},{10,8},{12,10},{14,12},{16,14},{18,16},{20... | collective-permute-start | bytes 392 | tf_op jit(solution)/shard_map/ppermute | solution.py:17
where the time goes:
time: 98.5 us; the launch traced here: 98 us
  starting transfers between devices  46.8 us (48%)
  waiting for transfers between devices  28.4 us (29%)
  local copies, waits for them, and re-layouts  10.2 us (10%)
  matrix products  6.78 us (7%)
  other arithmetic  3.75 us (4%)
  blocking collectives  1.82 us (2%)
    all_to_all x1, waiting for transfers between devices, body(): lax.all_to_all(outgoing.reshape(owners, capacity, width), 'patch', split_...  27.1 us
    ppermute x2, starting transfers between devices, with_halo(): lax.ppermute(lax.slice_in_dim(block, 0, width, axis=dim), axis, backward)  16.2 us
    all_to_all x1, starting transfers between devices, body(): lax.all_to_all(outgoing.reshape(owners, capacity, width), 'patch', split_...  13.8 us
    all_to_all x1, starting transfers between devices, body(): lax.all_to_all(row_ids.reshape(owners, capacity), 'patch', split_axis=0,...  10.6 us
    ppermute x2, starting transfers between devices, with_halo(): lax.ppermute(lax.slice_in_dim(block, block.shape[dim] - width, None, axis...  6.29 us
    dot_general x1, matrix products, body(): jnp.einsum('cjkm,crm->cjrk', block_values, blocks, preferred_element_type...  5.65 us
  transfers between devices with their start and end apart: 6, of which 2 were waited for; matrix products, arithmetic and copies ran while one was open for 15% of the time, Pallas kernels for 0%

commit v1 on v0

v1 whole, which is shorter than its diff:
```python
import functools

import jax
import jax.numpy as jnp
from jax import lax
from jax.experimental import pallas as pl
from jax.experimental.pallas import tpu as pltpu
from jax.sharding import Mesh, PartitionSpec as P

LEVELS = 3
NX, NY, NZ, NC = 4, 4, 8, 2
PATCH = ("x", "y", "z")
ALL = ("x", "y", "z", "c")
OWNERS = NX * NY * NZ
REC = NZ + 1


def device_id(x, y, z, c):
    return ((x * NY + y) * NZ + z) * NC + c


def halo_pairs():
    pairs = []
    for p in range(OWNERS):
        pairs.append((p * NC, ((p + 1) % OWNERS) * NC))
        pairs.append((p * NC + 1, ((p - 1) % OWNERS) * NC + 1))
    return pairs


def line_pairs(shift, swap):
    pairs = []
    for x in range(NX):
        for y in range(NY):
            for z in range(NZ):
                for c in range(NC):
                    if (c == 0) != swap:
                        target = device_id((x + shift) % NX, y, z, c)
                    else:
                        target = device_id(x, (y + shift) % NY, z, c)
                    pairs.append((device_id(x, y, z, c), target))
    return pairs


def inside_mask(length, margin):
    where = (
        lax.axis_index(PATCH) * length + jnp.arange(length + 2 * margin, dtype=jnp.int32) - margin
    )
    valid = (where >= 0) & (where < OWNERS * length)
    return valid.astype(jnp.float32)[None, :]


def forward(density, left, right):
    local_len = density.shape[1]
    reach = 2 ** (LEVELS + 1)
    details = []
    smooth = jnp.concatenate([left[:, -reach:], density, right[:, :reach]], axis=1)
    for level_index in range(LEVELS):
        margin = reach // 2 ** (level_index + 1)
        length = local_len // 2 ** (level_index + 1)
        keep = inside_mask(length, margin)
        even_part = smooth[:, 0::2]
        odd_part = smooth[:, 1::2]
        zero_col = jnp.zeros_like(even_part[:, :1])
        even_next = jnp.concatenate([even_part[:, 1:], zero_col], axis=1)
        detail = (odd_part - 0.5 * (even_part + even_next)) * keep
        detail_prior = jnp.concatenate([zero_col, detail[:, :-1]], axis=1)
        smooth = (even_part + 0.25 * (detail_prior + detail)) * keep
        details.append(detail[:, margin : margin + length])
    smooth = smooth[:, margin : margin + length]
    return jnp.concatenate([smooth] + details[::-1], axis=1).astype(jnp.bfloat16)


def inverse(pieces, lefts, rights):
    sides = pieces[0].shape[0]
    zero = jnp.zeros((sides, 1), jnp.float32)
    extended = [
        jnp.concatenate([zero, left, piece, right, zero], axis=1)
        for left, piece, right in zip(lefts, pieces, rights)
    ]
    smooth = extended[0]
    for step_index in range(LEVELS):
        detail = extended[step_index + 1]
        length = detail.shape[1] - 4
        keep = inside_mask(length, 2)
        zero_col = jnp.zeros_like(detail[:, :1])
        detail_prior = jnp.concatenate([zero_col, detail[:, :-1]], axis=1)
        even_part = (smooth - 0.25 * (detail_prior + detail)) * keep
        even_next = jnp.concatenate([even_part[:, 1:], zero_col], axis=1)
        odd_part = detail + 0.5 * (even_part + even_next)
        smooth = jnp.stack([even_part, odd_part], axis=-1).reshape(sides, -1)[:, 2:-2]
    return smooth[:, 2:-2]


def terms_kernel(counts, core, vector, values, own, other):
    step = pl.program_id(0)
    chunk = values.shape[0]
    slots = (pl.num_programs(0) * chunk) // vector.shape[0]
    column = (step * chunk) // slots
    first = (step * chunk) % slots + core[0] * slots
    vec = vector[column]
    for index in range(chunk):
        term = lax.dot_general(
            vec, values[index], (((1,), (1,)), ((), ())), preferred_element_type=jnp.float32
        )
        term = jnp.where(first + index < counts[column], term[:4], 0.0)
        low, high = term[:, :128], term[:, 128:]
        own[index] = jnp.where(core[0] == 0, low, high)
        other[index] = jnp.where(core[0] == 0, high, low)


def terms(vector, values, counts, core):
    held = values.shape[0]
    chunk = 8
    smem = pl.BlockSpec(memory_space=pltpu.SMEM)
    block = jax.ShapeDtypeStruct((held, 4, 128), jnp.float32)
    return pl.pallas_call(
        terms_kernel,
        grid=(held // chunk,),
        in_specs=[
            smem,
            smem,
            pl.BlockSpec(vector.shape, lambda i: (0, 0, 0)),
            pl.BlockSpec((chunk, 256, 256), lambda i: (i, 0, 0)),
        ],
        out_specs=[pl.BlockSpec((chunk, 4, 128), lambda i: (i, 0, 0))] * 2,
        out_shape=[block, block],
        name="terms",
    )(counts, core, vector, values)


def relative(column_x, column_y, place):
    first = jnp.where(place[2] == 0, column_x - place[0], column_y - place[1])
    second = jnp.where(place[2] == 0, column_y - place[1], column_x - place[0])
    return (first & 3) * 4 + (second & 3)


def scatter_kernel(place, rows_own, rows_other, own, other, out0, out1, out2, out3, dense):
    dense[...] = jnp.zeros_like(dense)
    for rows, source in ((rows_own, own), (rows_other, other)):

        def add(index, carry):
            row = rows[index]
            owner = row >> 2
            column = relative(owner >> 5, (owner >> 3) & 3, place)
            spot = (column * REC + (owner & 7)) * 4 + (row & 3)
            dense[spot] = dense[spot] + source[index]
            return carry

        lax.fori_loop(0, source.shape[0], add, 0, unroll=8)
    lane = lax.broadcasted_iota(jnp.int32, (4, 128), 1)
    for first in range(4):
        for second in range(4):
            here = first * 4 + second
            x = (jnp.where(place[2] == 0, first, second) + place[0]) & 3
            y = (jnp.where(place[2] == 0, second, first) + place[1]) & 3
            column = x * 4 + y
            after = (column + 1) & 15
            before = (column + 15) & 15
            right = relative(after >> 2, after & 3, place) * REC * 4
            left = (relative(before >> 2, before & 3, place) * REC + 7) * 4
            for b in range(4):
                high = jnp.where(column == 15, 0.0, dense[right + b])
                low = jnp.where(column == 0, 0.0, dense[left + b])
                dense[(here * REC + NZ) * 4 + b] = jnp.where(lane < 64, high, low)
    size = out0.shape[0]
    for index, out in enumerate((out0, out1, out2, out3)):
        out[...] = dense[pl.ds(index * size, size)]


def scatter(place, rows_own, rows_other, own, other):
    size = 4 * REC * 4
    smem = pl.BlockSpec(memory_space=pltpu.SMEM)
    vmem = pl.BlockSpec(memory_space=pltpu.VMEM)
    return pl.pallas_call(
        scatter_kernel,
        in_specs=[smem] * 3 + [vmem] * 2,
        out_specs=[vmem] * 4,
        out_shape=[jax.ShapeDtypeStruct((size, 4, 128), jnp.float32)] * 4,
        scratch_shapes=[pltpu.VMEM((4 * size, 4, 128), jnp.float32)],
        name="scatter",
    )(place, rows_own, rows_other, own, other)


def body(density, block_values, block_rows, block_counts):
    sides, local_len = density.shape
    col_blocks, slots, block, _ = block_values.shape
    held = col_blocks * slots
    x, y, z, c = (lax.axis_index(axis) for axis in ALL)
    patch = lax.axis_index(PATCH)
    across = [(0, 1), (1, 0)]
    edge = jnp.where(c == 0, density[:, -128:], density[:, :128])
    halo = lax.ppermute(edge, ALL, halo_pairs())
    ids = jnp.concatenate(
        [block_rows.reshape(1, held).astype(jnp.float32), jnp.zeros((1, 128 - held), jnp.float32)], axis=1
    )
    swapped = lax.ppermute(jnp.concatenate([halo, ids], axis=0), "c", across)
    rows_other = swapped[4, :held].astype(jnp.int32)
    rows_own = block_rows.reshape(held)
    left = jnp.where(c == 0, halo, swapped[:4]) * (patch > 0).astype(jnp.float32)
    right = jnp.where(c == 0, swapped[:4], halo) * (patch < OWNERS - 1).astype(jnp.float32)

    vector = forward(density, left, right)
    blocks = vector.reshape(sides, col_blocks, block).transpose(1, 0, 2)
    blocks = jnp.concatenate([blocks, jnp.zeros_like(blocks)], axis=1)
    core = c.reshape(1).astype(jnp.int32)
    own, other = terms(blocks, block_values.reshape(held, block, block), block_counts, core)
    received = lax.ppermute(other, "c", across)
    place = jnp.stack([x, y, c]).astype(jnp.int32)
    parts = scatter(place, rows_own, rows_other, own, received)

    first = parts[0]
    for shift in (2, 1, 3):
        first = first + lax.ppermute(parts[shift], ALL, line_pairs(shift, False))
    first = first.reshape(4, REC, 16, 128)
    second = first[0]
    for shift in (2, 1, 3):
        second = second + lax.ppermute(first[shift], ALL, line_pairs(shift, True))
    lane = jnp.arange(128, dtype=jnp.int32)[None, None, :]
    ends = second[NZ:]
    mine = second[:NZ]
    after = jnp.concatenate([mine[1:], ends], axis=0)
    before = jnp.concatenate([ends, mine[:-1]], axis=0)
    message = jnp.concatenate([mine, jnp.where(lane < 64, after, before)], axis=1)
    last = lax.all_to_all(message, "z", 0, 0, tiled=True).sum(axis=0)
    peer = lax.ppermute(last, "c", across)
    zero_half = jnp.where(c == 0, last, peer).reshape(2, 4, 4, 128)
    one_half = jnp.where(c == 0, peer, last).reshape(2, 4, 4, 128)
    a, ga = zero_half[0], zero_half[1]
    d, gd = one_half[0], one_half[1]
    pieces = [
        a[0],
        d[0],
        jnp.concatenate([a[1], d[1]], axis=1),
        jnp.concatenate([a[2], d[2], a[3], d[3]], axis=1),
    ]
    zero = jnp.zeros((sides, 1), jnp.float32)
    lefts = [zero, gd[0][:, 127:], gd[1][:, 127:], gd[3][:, 127:]]
    rights = [ga[0][:, :1], gd[0][:, :1], ga[1][:, :1], ga[2][:, :1]]
    return 0.5 * density + inverse(pieces, lefts, rights)


def solution(mesh):
    grid = Mesh(mesh.devices.reshape(NX, NY, NZ, NC), ALL)
    return jax.shard_map(
        body,
        mesh=grid,
        in_specs=(P(None, PATCH), P(PATCH, "c", None, None), P(PATCH, "c"), P(PATCH)),
        out_specs=P(None, PATCH),
        check_vma=False,
    )
```

time: 98.5 us -> 74.5 us (0.76)
  the two profiles are of different devices: /device:TPU:6 before, /device:TPU:1 now
where the time goes in v1:
time: 74.5 us; the launch traced here: 74 us
  starting transfers between devices  28.3 us (38%)
  waiting for transfers between devices  20.7 us (28%)
  Pallas kernels  11.2 us (15%)
  local copies, waits for them, and re-layouts  7.83 us (11%)
  other arithmetic  5.75 us (8%)
    ppermute x1, starting transfers between devices, body(): halo = lax.ppermute(edge, ALL, halo_pairs())  11 us
    ppermute x3, waiting for transfers between devices, body(): first = first + lax.ppermute(parts[shift], ALL, line_pairs(shift, False))  8.98 us
    pallas_call x1, Pallas kernels, terms(): pl.pallas_call(terms_kernel, grid=(held // chunk,), in_specs=[smem, smem,...  7.95 us
    all_to_all x1, waiting for transfers between devices, body(): last = lax.all_to_all(message, 'z', 0, 0, tiled=True).sum(axis=0)  7.94 us
    all_to_all x1, starting transfers between devices, body(): last = lax.all_to_all(message, 'z', 0, 0, tiled=True).sum(axis=0)  5.62 us
    ppermute x1, starting transfers between devices, body(): peer = lax.ppermute(last, 'c', across)  4.7 us
    ppermute x3, starting transfers between devices, body(): second = second + lax.ppermute(first[shift], ALL, line_pairs(shift, True))  3.63 us
    pallas_call x1, Pallas kernels, scatter(): pl.pallas_call(scatter_kernel, in_specs=[smem] * 3 + [vmem] * 2, out_spec...  3.25 us
  transfers between devices with their start and end apart: 11, of which 7 were waited for; matrix products, arithmetic and copies ran while one was open for 4% of the time, Pallas kernels for 0%

profile of v1, /device:TPU:1, one launch (start us, length us, event | category | flops | bytes accessed | tf_op | source)
XLA Modules:
  0.0 74.0 jit_solution(13196229870881055838)
XLA Ops:
  0.0 0.7 slice_select_fusion.1
  0.7 11.0 %collective-permute-start = (f32[4,128]{1,0:T(4,128)S(1)}, f32[4,128]{1,0:T(4,128)S(1)}, u32[]{:S(2)}, u32[]{:S(2)}) collective-permute-start(f32[4,128]{1,0:T(4,128)S(1)} %slice_select_fusion.1), channel_id=1, source_target_pairs={{0,2},{1,255},{2,4},{3,1},{4,6},{5,3},{6,8},{7,5},{8,10},{9,7},{10... | collective-permute-start | bytes 6152 | tf_op jit(solution)/shard_map/ppermute | solution.py:192
  11.8 0.7 convert_element_type.66
  12.6 1.8 %collective-permute-start.1 = (f32[5,128]{1,0:T(8,128)S(1)}, f32[5,128]{1,0:T(8,128)S(1)}, u32[]{:S(2)}, u32[]{:S(2)}) collective-permute-start(f32[5,128]{1,0:T(8,128)S(1)} %select_maximum_fusion.3), channel_id=1, source_target_pairs={{0,1},{1,0},{2,3},{3,2},{4,5},{5,4},{6,7},{7,6},{8,9},{9,8},{10,11... | collective-permute-start | bytes 7688 | tf_op jit(solution)/shard_map/ppermute | solution.py:196
  14.4 0.6 pad_add_fusion.1.place
  15.0 1.3 %reshape.131.rows_own = s32[64]{0:T(128)} reshape(s32[4,16]{1,0:T(4,128)} %param.6) | data formatting | bytes 512 | tf_op jit(solution)/shard_map/reshape | solution.py:198
  16.4 0.8 %concatenate.84 = f32[4,1056]{1,0:T(4,128)S(1)} concatenate(f32[4,16]{1,0:T(4,128)S(1)} %slice.225, f32[4,1024]{1,0:T(4,128)} %param.4, f32[4,16]{1,0:T(4,128)S(1)} %bitcast.60), dimensions={1} | concatenate | bytes 33792 | tf_op jit(solution)/shard_map/concatenate | solution.py:56
  17.3 0.4 slice.227
  17.6 0.4 slice.228
  18.4 0.2 slice.232
  19.7 0.6 concatenate.92.vector
  20.3 8.0 %terms.1 = (f32[64,4,128]{2,1,0:T(4,128)}, f32[64,4,128]{2,1,0:T(4,128)}) custom-call(s32[4]{0:T(128)} %counts.1, s32[1]{0:T(128)} %bitcast.2.core, bf16[4,8,256]{2,1,0:T(8,128)(2,1)} %concatenate.92.vector, bf16[64,256,256]{2,1,0:T(8,128)(2,1)} %bitcast.40), custom_call_target="tpu_custom_call" | custom-call | tf_op jit(solution)/shard_map/terms/pallas_call | solution.py:116
  28.3 0.5 convert_bitcast_fusion.rows_other
  28.8 1.0 %collective-permute-done.2.other = f32[64,4,128]{2,1,0:T(4,128)S(1)} collective-permute-done((f32[64,4,128]{2,1,0:T(4,128)}, f32[64,4,128]{2,1,0:T(4,128)S(1)}, u32[]{:S(2)}, u32[]{:S(2)}) %collective-permute-start.2) | collective-permute-done | bytes 131104 | tf_op jit(solution)/shard_map/ppermute | solution.py:207
  29.8 0.6 copy-done
  30.5 3.2 %scatter.1 = (f32[144,4,128]{2,1,0:T(4,128)}, f32[144,4,128]{2,1,0:T(4,128)}, f32[144,4,128]{2,1,0:T(4,128)}, f32[144,4,128]{2,1,0:T(4,128)}) custom-call(s32[3]{0:T(128)} %pad_add_fusion.1.place, s32[64]{0:T(128)} %reshape.131.rows_own, s32[64]{0:T(128)} %convert_bitcast_fusion.rows_other, f32[64,4,128]{2,1,0:T(4,128)} %get-tuple-element.11.own, ...), custom_call_target="tpu_custom_call" | custom-call | tf_op jit(solution)/shard_map/scatter/pallas_call | solution.py:174
  33.7 1.5 %collective-permute-start.4 = (f32[144,4,128]{2,1,0:T(4,128)}, f32[144,4,128]{2,1,0:T(4,128)S(1)}, u32[]{:S(2)}, u32[]{:S(2)}) collective-permute-start(f32[144,4,128]{2,1,0:T(4,128)} %get-tuple-element.15), channel_id=1, source_target_pairs={{0,64},{1,17},{2,66},{3,19},{4,68},{5,21},{6,70},{7,23},{8,72},{9,... | collective-permute-start | bytes 884744 | tf_op jit(solution)/shard_map/ppermute | solution.py:213
  35.2 4.6 %collective-permute-done.5 = f32[144,4,128]{2,1,0:T(4,128)S(1)} collective-permute-done((f32[144,4,128]{2,1,0:T(4,128)}, f32[144,4,128]{2,1,0:T(4,128)S(1)}, u32[]{:S(2)}, u32[]{:S(2)}) %collective-permute-start.5) | collective-permute-done | bytes 294944 | tf_op jit(solution)/shard_map/ppermute | solution.py:213
  39.8 4.4 %collective-permute-done.4 = f32[144,4,128]{2,1,0:T(4,128)S(1)} collective-permute-done((f32[144,4,128]{2,1,0:T(4,128)}, f32[144,4,128]{2,1,0:T(4,128)S(1)}, u32[]{:S(2)}, u32[]{:S(2)}) %collective-permute-start.4) | collective-permute-done | bytes 294944 | tf_op jit(solution)/shard_map/ppermute | solution.py:213
  44.2 1.1 %add_add_fusion = f32[72,8,128]{2,1,0:T(8,128)S(1)} fusion(f32[72,8,128]{2,1,0:T(8,128)S(1)} %bitcast.49, f32[72,8,128]{2,1,0:T(8,128)S(1)} %bitcast.50, f32[72,8,128]{2,1,0:T(8,128)} %bitcast.48, f32[72,8,128]{2,1,0:T(8,128)S(1)} %bitcast.51), kind=kLoop, calls=%fused_computation.1 | loop fusion | flops 221184 | bytes 1474560 | tf_op jit(solution)/shard_map/add | solution.py:213
  45.3 0.9 %collective-permute-start.6 = (f32[9,16,128]{2,1,0:T(8,128)S(1)}, f32[9,16,128]{2,1,0:T(8,128)S(1)}, u32[]{:S(2)}, u32[]{:S(2)}) collective-permute-start(f32[9,16,128]{2,1,0:T(8,128)S(1)} %bitcast.55), channel_id=1, source_target_pairs={{0,32},{1,129},{2,34},{3,131},{4,36},{5,133},{6,38},{7,135},{8,40}... | collective-permute-start | bytes 221192 | tf_op jit(solution)/shard_map/ppermute | solution.py:217
  46.2 0.5 collective-permute-start.7
  46.7 2.2 %collective-permute-start.8 = (f32[9,16,128]{2,1,0:T(8,128)S(1)}, f32[9,16,128]{2,1,0:T(8,128)S(1)}, u32[]{:S(2)}, u32[]{:S(2)}) collective-permute-start(f32[9,16,128]{2,1,0:T(8,128)S(1)} %bitcast.53), channel_id=1, source_target_pairs={{0,48},{1,193},{2,50},{3,195},{4,52},{5,197},{6,54},{7,199},{8,56}... | collective-permute-start | bytes 221192 | tf_op jit(solution)/shard_map/ppermute | solution.py:217
  48.9 1.2 %collective-permute-done.6 = f32[9,16,128]{2,1,0:T(8,128)S(1)} collective-permute-done((f32[9,16,128]{2,1,0:T(8,128)S(1)}, f32[9,16,128]{2,1,0:T(8,128)S(1)}, u32[]{:S(2)}, u32[]{:S(2)}) %collective-permute-start.6) | collective-permute-done | bytes 73760 | tf_op jit(solution)/shard_map/ppermute | solution.py:217
  50.1 0.8 %collective-permute-done.7 = f32[9,16,128]{2,1,0:T(8,128)S(1)} collective-permute-done((f32[9,16,128]{2,1,0:T(8,128)S(1)}, f32[9,16,128]{2,1,0:T(8,128)S(1)}, u32[]{:S(2)}, u32[]{:S(2)}) %collective-permute-start.7) | collective-permute-done | bytes 73760 | tf_op jit(solution)/shard_map/ppermute | solution.py:217
  50.9 0.7 pad_maximum_fusion.2
  51.6 5.6 %all-to-all-start = ((f32[8,32,128]{2,1,0:T(8,128)}), f32[8,32,128]{2,1,0:T(8,128)S(1)}, u32[]{:S(2)}, u32[]{:S(2)}) async-start(f32[8,32,128]{2,1,0:T(8,128)} %pad_maximum_fusion.2), calls=%async_computation | async-start | bytes 262144 | tf_op jit(solution)/shard_map/all_to_all | solution.py:224
  57.2 7.9 %all-to-all-done = f32[8,32,128]{2,1,0:T(8,128)S(1)} async-done(((f32[8,32,128]{2,1,0:T(8,128)}), f32[8,32,128]{2,1,0:T(8,128)S(1)}, u32[]{:S(2)}, u32[]{:S(2)}) %all-to-all-start) | async-done | bytes 131104 | tf_op jit(solution)/shard_map/all_to_all | solution.py:224
  65.2 4.7 %collective-permute-start.9 = (f32[32,128]{1,0:T(8,128)S(1)}, f32[32,128]{1,0:T(8,128)S(1)}, u32[]{:S(2)}, u32[]{:S(2)}) collective-permute-start(f32[32,128]{1,0:T(8,128)S(1)} %reduce_sum.9), channel_id=1, source_target_pairs={{0,1},{1,0},{2,3},{3,2},{4,5},{5,4},{6,7},{7,6},{8,9},{9,8},{10,11... | collective-permute-start | bytes 49160 | tf_op jit(solution)/shard_map/ppermute | solution.py:225
  69.9 0.8 %collective-permute-done.9 = f32[32,128]{1,0:T(8,128)S(1)} collective-permute-done((f32[32,128]{1,0:T(8,128)S(1)}, f32[32,128]{1,0:T(8,128)S(1)}, u32[]{:S(2)}, u32[]{:S(2)}) %collective-permute-start.9) | collective-permute-done | bytes 16416 | tf_op jit(solution)/shard_map/ppermute | solution.py:225
  72.9 0.3 copy.67
  73.4 0.6 multiply_add_fusion
  (74 shorter events, 4.1 us)
Async XLA Ops:
  0.7 11.8 %collective-permute-start = (f32[4,128]{1,0:T(4,128)S(1)}, f32[4,128]{1,0:T(4,128)S(1)}, u32[]{:S(2)}, u32[]{:S(2)}) collective-permute-start(f32[4,128]{1,0:T(4,128)S(1)} %slice_select_fusion.1), channel_id=1, source_target_pairs={{0,2},{1,255},{2,4},{3,1},{4,6},{5,3},{6,8},{7,5},{8,10},{9,7},{10... | collective-permute-start | bytes 6152 | tf_op jit(solution)/shard_map/ppermute | solution.py:192
  12.6 3.8 %collective-permute-start.1 = (f32[5,128]{1,0:T(8,128)S(1)}, f32[5,128]{1,0:T(8,128)S(1)}, u32[]{:S(2)}, u32[]{:S(2)}) collective-permute-start(f32[5,128]{1,0:T(8,128)S(1)} %select_maximum_fusion.3), channel_id=1, source_target_pairs={{0,1},{1,0},{2,3},{3,2},{4,5},{5,4},{6,7},{7,6},{8,9},{9,8},{10,11... | collective-permute-start | bytes 7688 | tf_op jit(solution)/shard_map/ppermute | solution.py:196
  28.3 45.1 %copy-start.1 = (f32[4,1024]{1,0:T(4,128)S(1)}, f32[4,1024]{1,0:T(4,128)}, u32[]{:S(2)}) copy-start(f32[4,1024]{1,0:T(4,128)} %param.4) | copy-start | bytes 49156
  28.3 1.6 %collective-permute-start.2 = (f32[64,4,128]{2,1,0:T(4,128)}, f32[64,4,128]{2,1,0:T(4,128)S(1)}, u32[]{:S(2)}, u32[]{:S(2)}) collective-permute-start(f32[64,4,128]{2,1,0:T(4,128)} %get-tuple-element.12), channel_id=1, source_target_pairs={{0,1},{1,0},{2,3},{3,2},{4,5},{5,4},{6,7},{7,6},{8,9},{9,8},{10,11... | collective-permute-start | bytes 393224 | tf_op jit(solution)/shard_map/ppermute | solution.py:207
  29.8 0.6 copy-start
  33.7 6.1 %collective-permute-start.5 = (f32[144,4,128]{2,1,0:T(4,128)}, f32[144,4,128]{2,1,0:T(4,128)S(1)}, u32[]{:S(2)}, u32[]{:S(2)}) collective-permute-start(f32[144,4,128]{2,1,0:T(4,128)} %get-tuple-element.16), channel_id=1, source_target_pairs={{0,192},{1,49},{2,194},{3,51},{4,196},{5,53},{6,198},{7,55},{8,200... | collective-permute-start | bytes 884744 | tf_op jit(solution)/shard_map/ppermute | solution.py:213
  33.7 10.4 %collective-permute-start.4 = (f32[144,4,128]{2,1,0:T(4,128)}, f32[144,4,128]{2,1,0:T(4,128)S(1)}, u32[]{:S(2)}, u32[]{:S(2)}) collective-permute-start(f32[144,4,128]{2,1,0:T(4,128)} %get-tuple-element.15), channel_id=1, source_target_pairs={{0,64},{1,17},{2,66},{3,19},{4,68},{5,21},{6,70},{7,23},{8,72},{9,... | collective-permute-start | bytes 884744 | tf_op jit(solution)/shard_map/ppermute | solution.py:213
  35.2 9.0 %collective-permute-start.3 = (f32[144,4,128]{2,1,0:T(4,128)}, f32[144,4,128]{2,1,0:T(4,128)S(1)}, u32[]{:S(2)}, u32[]{:S(2)}) collective-permute-start(f32[144,4,128]{2,1,0:T(4,128)} %get-tuple-element.14), channel_id=1, source_target_pairs={{0,128},{1,33},{2,130},{3,35},{4,132},{5,37},{6,134},{7,39},{8,136... | collective-permute-start | bytes 884744 | tf_op jit(solution)/shard_map/ppermute | solution.py:213
  45.3 4.8 %collective-permute-start.6 = (f32[9,16,128]{2,1,0:T(8,128)S(1)}, f32[9,16,128]{2,1,0:T(8,128)S(1)}, u32[]{:S(2)}, u32[]{:S(2)}) collective-permute-start(f32[9,16,128]{2,1,0:T(8,128)S(1)} %bitcast.55), channel_id=1, source_target_pairs={{0,32},{1,129},{2,34},{3,131},{4,36},{5,133},{6,38},{7,135},{8,40}... | collective-permute-start | bytes 221192 | tf_op jit(solution)/shard_map/ppermute | solution.py:217
  46.2 4.6 %collective-permute-start.7 = (f32[9,16,128]{2,1,0:T(8,128)S(1)}, f32[9,16,128]{2,1,0:T(8,128)S(1)}, u32[]{:S(2)}, u32[]{:S(2)}) collective-permute-start(f32[9,16,128]{2,1,0:T(8,128)S(1)} %bitcast.54), channel_id=1, source_target_pairs={{0,16},{1,65},{2,18},{3,67},{4,20},{5,69},{6,22},{7,71},{8,24},{9,... | collective-permute-start | bytes 221192 | tf_op jit(solution)/shard_map/ppermute | solution.py:217
  46.7 4.2 %collective-permute-start.8 = (f32[9,16,128]{2,1,0:T(8,128)S(1)}, f32[9,16,128]{2,1,0:T(8,128)S(1)}, u32[]{:S(2)}, u32[]{:S(2)}) collective-permute-start(f32[9,16,128]{2,1,0:T(8,128)S(1)} %bitcast.53), channel_id=1, source_target_pairs={{0,48},{1,193},{2,50},{3,195},{4,52},{5,197},{6,54},{7,199},{8,56}... | collective-permute-start | bytes 221192 | tf_op jit(solution)/shard_map/ppermute | solution.py:217
  51.6 13.6 %all-to-all-start = ((f32[8,32,128]{2,1,0:T(8,128)}), f32[8,32,128]{2,1,0:T(8,128)S(1)}, u32[]{:S(2)}, u32[]{:S(2)}) async-start(f32[8,32,128]{2,1,0:T(8,128)} %pad_maximum_fusion.2), calls=%async_computation | async-start | bytes 262144 | tf_op jit(solution)/shard_map/all_to_all | solution.py:224
  65.2 5.5 %collective-permute-start.9 = (f32[32,128]{1,0:T(8,128)S(1)}, f32[32,128]{1,0:T(8,128)S(1)}, u32[]{:S(2)}, u32[]{:S(2)}) collective-permute-start(f32[32,128]{1,0:T(8,128)S(1)} %reduce_sum.9), channel_id=1, source_target_pairs={{0,1},{1,0},{2,3},{3,2},{4,5},{5,4},{6,7},{7,6},{8,9},{9,8},{10,11... | collective-permute-start | bytes 49160 | tf_op jit(solution)/shard_map/ppermute | solution.py:225

commit v2 on v0

v2 whole, which is shorter than its diff:
```python
import jax
import jax.numpy as jnp
import numpy as np
from jax import lax
from jax.experimental import pallas as pl
from jax.experimental.pallas import tpu as pltpu
from jax.sharding import Mesh, PartitionSpec as P

LEVELS = 3
NX, NY, NZ, NC = 4, 4, 8, 2
PATCH = ("x", "y", "z")
ALL = ("x", "y", "z", "c")
OWNERS = NX * NY * NZ
TILES = 2 * NZ + 2
COLS, SLOTS, BS = 4, 16, 256
HELD = COLS * SLOTS
LEN = COLS * BS
REACH = 16
SMALL = 4 * 1024 * 1024


def device_id(x, y, z, c):
    return ((x * NY + y) * NZ + z) * NC + c


def halo_pairs():
    pairs = []
    for p in range(OWNERS):
        pairs.append((p * NC, ((p + 1) % OWNERS) * NC))
        pairs.append((p * NC + 1, ((p - 1) % OWNERS) * NC + 1))
    return pairs


def line_pairs(shift, swap):
    pairs = []
    for x in range(NX):
        for y in range(NY):
            for z in range(NZ):
                for c in range(NC):
                    if (c == 0) != swap:
                        target = device_id((x + shift) % NX, y, z, c)
                    else:
                        target = device_id(x, (y + shift) % NY, z, c)
                    pairs.append((device_id(x, y, z, c), target))
    return pairs


def edge_table():
    table = np.zeros((128, 128), np.float32)
    for at_end in (False, True):
        for unit in range(64):
            line = np.zeros(LEN + 2 * REACH)
            where = unit if unit < 32 else LEN + unit - 32
            line[where] = 1.0
            if at_end:
                line[:REACH] = 0.0
                line[REACH + LEN :] = 0.0
            smooth, details = line, []
            for level in range(LEVELS):
                margin, length = REACH >> (level + 1), LEN >> (level + 1)
                keep = np.ones(length + 2 * margin)
                if at_end:
                    keep[:margin] = 0.0
                    keep[margin + length :] = 0.0
                even, odd = smooth[0::2], smooth[1::2]
                detail = (odd - 0.5 * (even + np.append(even[1:], 0.0))) * keep
                smooth = (even + 0.25 * (np.append(0.0, detail[:-1]) + detail)) * keep
                details.append(detail[margin : margin + length])
            s3 = smooth[margin : margin + length]
            d1, d2, d3 = details
            values = [s3[0], d3[0], d3[127], d2[0], d2[255], d1[511]]
            table[unit, 8 * at_end : 8 * at_end + 6] = values
    return table


def coordinates():
    return [lax.axis_index(axis) for axis in ALL]


def terms_kernel(counts, density, values, own, send, wide, xt, d1, s1, d2, s2, d3, vec, acc, held, sems):
    core = lax.axis_index("c")
    parts = 8
    size = HELD // parts
    copies = [
        pltpu.make_async_copy(values.at[pl.ds(i * size, size)], held.at[pl.ds(i * size, size)], sems.at[i])
        for i in range(parts)
    ]
    for copy in copies:
        copy.start()
    wide[0:4, :] = density[...]
    wide[4:8, :] = density[...]
    for group in range(8):
        tile = wide[:, pl.ds(group * 128, 128)]
        xt[pl.ds(8 + group * 128, 128), :] = jnp.concatenate([tile] * 16, axis=0).T
    pad = jnp.zeros((8, 128), jnp.float32)

    def lift(source, length, detail, smooth, fix):
        source[pl.ds(8 + 2 * length, 8), :] = pad
        detail[0:8, :] = pad
        step = min(length, 128)
        for start in range(0, length, step):
            even = source[pl.ds(8 + 2 * start, step, stride=2), :]
            odd = source[pl.ds(9 + 2 * start, step, stride=2), :]
            after = source[pl.ds(10 + 2 * start, step, stride=2), :]
            detail[pl.ds(8 + start, step), :] = odd - 0.5 * (even + after)
        if fix:
            row = lax.broadcasted_iota(jnp.int32, (8, 128), 0)
            detail[8:16, :] = jnp.where(row == 0, 0.0, detail[8:16, :])
            detail[pl.ds(length, 8), :] = jnp.where(row == 7, 0.0, detail[pl.ds(length, 8), :])
        for start in range(0, length, step):
            even = source[pl.ds(8 + 2 * start, step, stride=2), :]
            low = detail[pl.ds(7 + start, step), :]
            high = detail[pl.ds(8 + start, step), :]
            smooth(start, step, even + 0.25 * (low + high))

    lane = lax.broadcasted_iota(jnp.int32, (8, 128), 1) & 7
    row = lax.broadcasted_iota(jnp.int32, (8, 128), 0)

    def put(at, value):
        count = value.shape[0]
        lanes = lax.broadcasted_iota(jnp.int32, (count, 128), 1) & 7
        vec[pl.ds(at, count), :] = jnp.where(lanes < 4, value, 0.0)

    def keep1(start, step, value):
        s1[pl.ds(8 + start, step), :] = value

    def keep2(start, step, value):
        s2[pl.ds(8 + start, step), :] = value

    lift(xt, 512, d1, keep1, False)
    lift(s1, 256, d2, keep2, False)
    lift(s2, 128, d3, lambda start, step, value: put(start, value), True)
    put(128, d3[8:136, :])
    put(256, d2[8:264, :])
    for start in range(0, 512, 128):
        put(512 + start, d1[pl.ds(8 + start, 128), :])

    def patch(at, which, lanes_weights, clear):
        tile = vec[pl.ds(at, 8), :]
        if clear:
            tile = jnp.where((row == which) & (lane < 4), 0.0, tile)
        for index, at_row, weight in lanes_weights:
            tile = jnp.where((row == at_row) & (lane == index), weight, tile)
        vec[pl.ds(at, 8), :] = tile

    patch(0, 0, [(4, 0, 1.0), (5, 1, 0.25)], True)
    patch(120, 7, [(6, 7, 0.25)], False)
    patch(128, 0, [(5, 0, 1.0)], True)
    patch(248, 7, [(6, 7, 1.0)], True)
    patch(256, 0, [(4, 0, 1.0)], True)
    patch(504, 7, [(5, 7, 1.0)], True)
    patch(1016, 7, [(4, 7, 1.0)], True)

    whose = lax.broadcasted_iota(jnp.int32, (1, 128), 1) >> 3
    for column in range(COLS):
        vector = vec[pl.ds(column * BS, BS), :].astype(jnp.bfloat16)
        total = None
        for slot in range(SLOTS):
            index = column * SLOTS + slot
            if index % size == 0:
                copies[index // size].wait()
            live = core * SLOTS + slot < counts[column]
            mask = (whose == jnp.where(live, slot, -1)).astype(jnp.float32).astype(jnp.bfloat16)
            part = jnp.dot(held[index], vector * mask, preferred_element_type=jnp.float32)
            if slot == 0:
                acc[...] = part
            else:
                acc[...] += part
        turned = acc[...].T
        low = turned[:, :128].reshape(SLOTS, 8, 128)
        high = turned[:, 128:].reshape(SLOTS, 8, 128)
        at = pl.ds(column * SLOTS, SLOTS)
        own[at] = jnp.where(core == 0, low, high)
        send[at] = jnp.where(core == 0, high, low)


def terms(counts, density, values):
    smem = pl.BlockSpec(memory_space=pltpu.SMEM)
    vmem = pl.BlockSpec(memory_space=pltpu.VMEM)
    block = jax.ShapeDtypeStruct((HELD, 8, 128), jnp.float32)
    f32 = jnp.float32
    return pl.pallas_call(
        terms_kernel,
        in_specs=[smem, vmem, pl.BlockSpec(memory_space=pltpu.HBM)],
        out_specs=[vmem, vmem],
        out_shape=[block, block],
        scratch_shapes=[
            pltpu.VMEM((8, LEN), f32),
            pltpu.VMEM((LEN + 16, 128), f32),
            pltpu.VMEM((512 + 16, 128), f32),
            pltpu.VMEM((512 + 16, 128), f32),
            pltpu.VMEM((256 + 16, 128), f32),
            pltpu.VMEM((256 + 16, 128), f32),
            pltpu.VMEM((128 + 16, 128), f32),
            pltpu.VMEM((LEN, 128), f32),
            pltpu.VMEM((BS, 128), f32),
            pltpu.VMEM((HELD, BS, BS), jnp.bfloat16),
            pltpu.SemaphoreType.DMA((8,)),
        ],
        compiler_params=pltpu.CompilerParams(vmem_limit_bytes=16 * 1024 * 1024),
        cost_estimate=pl.CostEstimate(
            flops=2 * HELD * BS * BS * 128, bytes_accessed=2 * HELD * BS * BS, transcendentals=0
        ),
        name="terms",
    )(counts, density, values)


def edges_kernel(density, mine, other, table, out):
    x, y, z, core = coordinates()
    left = jnp.where(core == 0, mine[...], other[...])
    right = jnp.where(core == 0, other[...], mine[...])
    lane = lax.broadcasted_iota(jnp.int32, (4, 128), 1)
    first = density[:, 0:128]
    last = density[:, LEN - 128 :]
    inputs = jnp.where(
        lane < 32,
        jnp.where(lane < 16, pltpu.roll(left, 16, 1), pltpu.roll(first, 16, 1)),
        jnp.where(lane < 48, pltpu.roll(last, 48, 1), pltpu.roll(right, 48, 1)),
    )
    inputs = jnp.where(lane < 64, inputs, 0.0)
    values = jnp.dot(
        inputs, table[...], precision=lax.Precision.HIGHEST, preferred_element_type=jnp.float32
    )
    patch = (x * NY + y) * NZ + z
    low = (lane == 0) | (lane == 1) | (lane == 3)
    at_end = jnp.where(low, (patch == 0).astype(jnp.int32), (patch == OWNERS - 1).astype(jnp.int32))
    values = jnp.where(at_end == 1, pltpu.roll(values, 120, 1), values)
    values = values.astype(jnp.bfloat16).astype(jnp.float32)
    for index in range(6):
        spread = jnp.broadcast_to(values[:, index : index + 1], (4, 128))
        out[index, 0:4, :] = spread
        out[index, 4:8, :] = jnp.zeros((4, 128), jnp.float32)


def edges(density, mine, other, table):
    vmem = pl.BlockSpec(memory_space=pltpu.VMEM)
    return pl.pallas_call(
        edges_kernel,
        in_specs=[vmem] * 4,
        out_specs=vmem,
        out_shape=jax.ShapeDtypeStruct((6, 8, 128), jnp.float32),
        compiler_params=pltpu.CompilerParams(vmem_limit_bytes=SMALL),
        cost_estimate=pl.CostEstimate(flops=10**6, bytes_accessed=10**5, transcendentals=0),
        name="edges",
    )(density, mine, other, table)


def scatter_kernel(rows_own, rows_other, own, other, edge, out0, out1, out2, out3, dense, staged, base):
    x, y, _, core = coordinates()

    def relative(column_x, column_y):
        dx, dy = (column_x - x) & 3, (column_y - y) & 3
        return jnp.where(core == 0, dx * 4 + dy, dy * 4 + dx)

    for column in range(16):
        base[column] = relative(column >> 2, column & 3) * TILES
    dense[...] = jnp.zeros_like(dense)
    sub = lax.broadcasted_iota(jnp.int32, (SLOTS, 8, 128), 1)
    which = ((0, 1, 2), (3, 4), (), (5,))
    for side, source in enumerate((own, other)):
        for column in range(COLS):
            tile = source[pl.ds(column * SLOTS, SLOTS)]
            total = tile
            for place, index in enumerate(which[column]):
                total = total + tile[:, 4 + place : 5 + place, :] * edge[index][None]
            total = jnp.where(sub < 4, total, 0.0)
            at = pl.ds((side * COLS + column) * SLOTS, SLOTS)
            staged[0, at] = total
            staged[1, at] = pltpu.roll(total, 4, 1)
    for side, rows in enumerate((rows_own, rows_other)):
        for column in range(COLS):
            for slot in range(SLOTS):
                number = rows[column, slot]
                spot = base[number >> 5] + ((number >> 1) & 15)
                value = staged[number & 1, (side * COLS + column) * SLOTS + slot]
                dense[spot] = dense[spot] + value
    lane = lax.broadcasted_iota(jnp.int32, (2, 8, 128), 2)
    for first in range(4):
        for second in range(4):
            here = (first * 4 + second) * TILES
            cx = (jnp.where(core == 0, first, second) + x) & 3
            cy = (jnp.where(core == 0, second, first) + y) & 3
            column = cx * 4 + cy
            high = jnp.where(column == 15, 0.0, dense[pl.ds(base[(column + 1) & 15], 2)])
            low = jnp.where(column == 0, 0.0, dense[pl.ds(base[(column + 15) & 15] + 14, 2)])
            dense[pl.ds(here + 2 * NZ, 2)] = jnp.where(lane < 64, high, low)
    size = 4 * TILES
    for index, out in enumerate((out0, out1, out2, out3)):
        out[...] = dense[pl.ds(index * size, size)]


def scatter(rows_own, rows_other, own, other, edge):
    size = 4 * TILES
    smem = pl.BlockSpec(memory_space=pltpu.SMEM)
    vmem = pl.BlockSpec(memory_space=pltpu.VMEM)
    return pl.pallas_call(
        scatter_kernel,
        in_specs=[smem] * 2 + [vmem] * 3,
        out_specs=[vmem] * 4,
        out_shape=[jax.ShapeDtypeStruct((size, 8, 128), jnp.float32)] * 4,
        scratch_shapes=[
            pltpu.VMEM((4 * size, 8, 128), jnp.float32),
            pltpu.VMEM((2, 2 * HELD, 8, 128), jnp.float32),
            pltpu.SMEM((16,), jnp.int32),
        ],
        compiler_params=pltpu.CompilerParams(vmem_limit_bytes=2 * SMALL),
        cost_estimate=pl.CostEstimate(flops=10**6, bytes_accessed=10**6, transcendentals=0),
        name="scatter",
    )(rows_own, rows_other, own, other, edge)


def messages_kernel(part0, part1, part2, part3, keep, send, total):
    z = lax.axis_index("z")
    total[...] = (part0[...] + part1[...]) + (part2[...] + part3[...])
    lane = lax.broadcasted_iota(jnp.int32, (2, 8, 128), 2)
    for out, parity in ((keep, z & 1), (send, 1 - (z & 1))):
        for index in range(4):
            owner = (((z >> 1) + index) & 3) * 2 + parity
            after = jnp.where(owner == NZ - 1, NZ, owner + 1)
            before = jnp.where(owner == 0, NZ, owner - 1)
            out[index, 0:2] = total[pl.ds(owner * 2, 2)]
            out[index, 2:4] = jnp.where(
                lane < 64, total[pl.ds(after * 2, 2)], total[pl.ds(before * 2, 2)]
            )


def messages(parts):
    vmem = pl.BlockSpec(memory_space=pltpu.VMEM)
    return pl.pallas_call(
        messages_kernel,
        in_specs=[vmem] * 4,
        out_specs=[vmem] * 2,
        out_shape=[jax.ShapeDtypeStruct((4, 4, 8, 128), jnp.float32)] * 2,
        scratch_shapes=[pltpu.VMEM((TILES, 8, 128), jnp.float32)],
        compiler_params=pltpu.CompilerParams(vmem_limit_bytes=SMALL),
        cost_estimate=pl.CostEstimate(flops=10**5, bytes_accessed=10**5, transcendentals=0),
        name="messages",
    )(*parts)


def inverse_kernel(density, mine, peer, out, turned, s3, s2, s1, s0, d3, d2, d1, even):
    x, y, z, core = coordinates()
    last = ((x * NY + y) * NZ + z) == OWNERS - 1
    inside = jnp.where(last, 0.0, 1.0)
    first = jnp.where(core == 0, mine[...], peer[...])
    second = jnp.where(core == 0, peer[...], mine[...])
    both = jnp.concatenate([first, second, jnp.zeros((64, 128), jnp.float32)], axis=0)
    turned[...] = both.T

    def piece(half, block):
        return pltpu.roll(turned[...], (128 - (half * 32 + block * 4)) % 128, 1)

    def ghost(half, block, top):
        tile = turned[0:8, :] if top else turned[120:128, :]
        return pltpu.roll(tile, (128 - (half * 32 + 16 + block * 4)) % 128, 1)

    def fill(target, length, parts, left, right):
        for index, (half, block) in enumerate(parts):
            target[pl.ds(8 + index * 128, 128), :] = piece(half, block)
        if left is not None:
            target[0:8, :] = ghost(left[0], left[1], False)
        target[pl.ds(8 + length, 8), :] = ghost(right[0], right[1], True)

    fill(s3, 128, [(0, 0)], None, (0, 0))
    fill(d3, 128, [(1, 0)], (1, 0), (1, 0))
    fill(d2, 256, [(0, 1), (1, 1)], (1, 1), (0, 1))
    fill(d1, 512, [(0, 2), (1, 2), (0, 3), (1, 3)], (1, 3), (0, 2))

    def level(smooth, detail, length, target):
        for start in range(0, length, 128):
            value = smooth[pl.ds(8 + start, 128), :] - 0.25 * (
                detail[pl.ds(7 + start, 128), :] + detail[pl.ds(8 + start, 128), :]
            )
            even[pl.ds(start, 128), :] = value
            target[pl.ds(8 + 2 * start, 128, stride=2), :] = value
        tail = inside * (
            smooth[pl.ds(8 + length, 8), :]
            - 0.25 * (detail[pl.ds(7 + length, 8), :] + detail[pl.ds(8 + length, 8), :])
        )
        even[pl.ds(length, 8), :] = tail
        target[pl.ds(8 + 2 * length, 8), :] = tail
        for start in range(0, length, 128):
            value = detail[pl.ds(8 + start, 128), :] + 0.5 * (
                even[pl.ds(start, 128), :] + even[pl.ds(start + 1, 128), :]
            )
            target[pl.ds(9 + 2 * start, 128, stride=2), :] = value

    level(s3, d3, 128, s2)
    level(s2, d2, 256, s1)
    level(s1, d1, 512, s0)
    for group in range(8):
        at = pl.ds(group * 128, 128)
        out[:, at] = 0.5 * density[:, at] + s0[pl.ds(8 + group * 128, 128), :].T[0:4, :]


def inverse(density, mine, peer):
    vmem = pl.BlockSpec(memory_space=pltpu.VMEM)
    f32 = jnp.float32
    return pl.pallas_call(
        inverse_kernel,
        in_specs=[vmem] * 3,
        out_specs=vmem,
        out_shape=jax.ShapeDtypeStruct(density.shape, f32),
        scratch_shapes=[pltpu.VMEM((128, 128), f32)]
        + [pltpu.VMEM((n + 16, 128), f32) for n in (128, 256, 512, 1024, 128, 256, 512, 512)],
        compiler_params=pltpu.CompilerParams(vmem_limit_bytes=2 * SMALL),
        cost_estimate=pl.CostEstimate(flops=10**6, bytes_accessed=10**5, transcendentals=0),
        name="inverse",
    )(density, mine, peer)


def body(density, block_values, block_rows, block_counts):
    core = lax.axis_index("c")
    across = [(0, 1), (1, 0)]
    edge = jnp.where(core == 0, density[:, -128:], density[:, :128])
    halo = lax.ppermute(edge, ALL, halo_pairs())
    rows_other = lax.ppermute(block_rows, "c", across)
    own, send = terms(block_counts, density, block_values.reshape(HELD, BS, BS))
    received = lax.ppermute(send, "c", across)
    halo_other = lax.ppermute(halo, "c", across)
    edge_values = edges(density, halo, halo_other, jnp.asarray(edge_table()))
    parts = scatter(block_rows, rows_other, own, received, edge_values)

    first = parts[0]
    for shift in (2, 1, 3):
        first = first + lax.ppermute(parts[shift], ALL, line_pairs(shift, False))
    first = first.reshape(4, TILES, 8, 128)
    second = [first[0]]
    for shift in (2, 1, 3):
        second.append(lax.ppermute(first[shift], ALL, line_pairs(shift, True)))
    keep, away = messages(second)
    keep = keep + lax.ppermute(away, "z", [(i, i ^ 1) for i in range(NZ)])
    last = keep[0]
    for shift in (2, 1, 3):
        last = last + lax.ppermute(keep[shift], "z", [(i, (i + 2 * shift) % NZ) for i in range(NZ)])
    last = last.reshape(32, 128)
    return inverse(density, last, lax.ppermute(last, "c", across))


def solution(mesh):
    grid = Mesh(mesh.devices.reshape(NX, NY, NZ, NC), ALL)
    return jax.shard_map(
        body,
        mesh=grid,
        in_specs=(P(None, PATCH), P(PATCH, "c", None, None), P(PATCH, "c"), P(PATCH)),
        out_specs=P(None, PATCH),
        check_vma=False,
    )
```

time: 98.5 us -> 62.1 us (0.63)
  the two profiles are of different devices: /device:TPU:6 before, /device:TPU:1 now
where the time goes in v2:
time: 62.1 us; the launch traced here: 61.9 us
  starting transfers between devices  28.6 us (46%)
  waiting for transfers between devices  20.1 us (32%)
  Pallas kernels  8.34 us (13%)
  local copies, waits for them, and re-layouts  4.79 us (8%)
    ppermute x1, starting transfers between devices, body(): halo = lax.ppermute(edge, ALL, halo_pairs())  8.51 us
    ppermute x3, waiting for transfers between devices, body(): first = first + lax.ppermute(parts[shift], ALL, line_pairs(shift, False))  7.56 us
    ppermute x3, starting transfers between devices, body(): lax.ppermute(keep[shift], 'z', [(i, (i + 2 * shift) % NZ) for i in range(...  5.48 us
    pallas_call x1, Pallas kernels, terms(): pl.pallas_call(terms_kernel, in_specs=[smem, vmem, pl.BlockSpec(memory_sp...  5.24 us
    ppermute x1, starting transfers between devices, body(): return inverse(density, last, lax.ppermute(last, 'c', across))  5.17 us
    unnamed x12, local copies, waits for them, and re-layouts  4.76 us
    ppermute x3, waiting for transfers between devices, body(): second.append(lax.ppermute(first[shift], ALL, line_pairs(shift, True)))  4.28 us
    ppermute x1, starting transfers between devices, body(): received = lax.ppermute(send, 'c', across)  3.29 us
  transfers between devices with their start and end apart: 15, of which 11 were waited for; matrix products, arithmetic and copies ran while one was open for 0% of the time, Pallas kernels for 1%

profile of v2, /device:TPU:1, one launch (start us, length us, event | category | flops | bytes accessed | tf_op | source)
XLA Modules:
  0.0 61.9 jit_solution(4432256172667111460)
XLA Ops:
  0.0 3.4 %copy-done = bf16[4,16,256,256]{3,2,1,0:T(8,128)(2,1)S(1)} copy-done((bf16[4,16,256,256]{3,2,1,0:T(8,128)(2,1)S(1)}, bf16[4,16,256,256]{3,2,1,0:T(8,128)(2,1)}, u32[]{:S(2)}) %copy-start) | copy-done | bytes 8388632
  3.4 0.7 %copy-done.1 = f32[4,1024]{1,0:T(4,128)S(1)} copy-done((f32[4,1024]{1,0:T(4,128)S(1)}, f32[4,1024]{1,0:T(4,128)}, u32[]{:S(2)}) %copy-start.1) | copy-done | bytes 16408
  4.1 0.7 %copy-done.5 = s32[4]{0:T(128)S(1)} copy-done((s32[4]{0:T(128)S(1)}, s32[4]{0:T(128)}, u32[]{:S(2)}) %copy-start.5) | copy-done | bytes 40
  4.8 5.2 %terms.1 = (f32[64,8,128]{2,1,0:T(8,128)S(1)}, f32[64,8,128]{2,1,0:T(8,128)S(1)}) custom-call(s32[4]{0:T(128)S(1)} %copy-done.5, f32[4,1024]{1,0:T(4,128)S(1)} %copy-done.1, bf16[64,256,256]{2,1,0:T(8,128)(2,1)S(1)} %bitcast.19), custom_call_target="tpu_custom_call" | custom-call | flops 1073741824 | bytes 8388608 | tf_op jit(solution)/shard_map/terms/pallas_call | solution.py:182
  10.0 3.3 %collective-permute-start.1 = (f32[64,8,128]{2,1,0:T(8,128)S(1)}, f32[64,8,128]{2,1,0:T(8,128)S(1)}, u32[]{:S(2)}, u32[]{:S(2)}) collective-permute-start(f32[64,8,128]{2,1,0:T(8,128)S(1)} %get-tuple-element.14), channel_id=1, source_target_pairs={{0,1},{1,0},{2,3},{3,2},{4,5},{5,4},{6,7},{7,6},{8,9},{9,8},{10,11... | collective-permute-start | bytes 786440 | tf_op jit(solution)/shard_map/ppermute | solution.py:419
  13.3 8.5 %collective-permute-start.2 = (f32[4,128]{1,0:T(4,128)S(1)}, f32[4,128]{1,0:T(4,128)S(1)}, u32[]{:S(2)}, u32[]{:S(2)}) collective-permute-start(f32[4,128]{1,0:T(4,128)S(1)} %slice_select_fusion), channel_id=1, source_target_pairs={{0,2},{1,255},{2,4},{3,1},{4,6},{5,3},{6,8},{7,5},{8,10},{9,7},{10... | collective-permute-start | bytes 6152 | tf_op jit(solution)/shard_map/ppermute | solution.py:416
  21.8 0.7 %collective-permute-done.2.mine = f32[4,128]{1,0:T(4,128)S(1)} collective-permute-done((f32[4,128]{1,0:T(4,128)S(1)}, f32[4,128]{1,0:T(4,128)S(1)}, u32[]{:S(2)}, u32[]{:S(2)}) %collective-permute-start.2) | collective-permute-done | bytes 2080 | tf_op jit(solution)/shard_map/ppermute | solution.py:416
  22.6 1.2 %collective-permute-start.3 = (f32[4,128]{1,0:T(4,128)S(1)}, f32[4,128]{1,0:T(4,128)S(1)}, u32[]{:S(2)}, u32[]{:S(2)}) collective-permute-start(f32[4,128]{1,0:T(4,128)S(1)} %collective-permute-done.2.mine), channel_id=1, source_target_pairs={{0,1},{1,0},{2,3},{3,2},{4,5},{5,4},{6,7},{7,6},{8,9},{9,8},{10,11... | collective-permute-start | bytes 6152 | tf_op jit(solution)/shard_map/ppermute | solution.py:420
  23.8 0.8 %collective-permute-done.3.other = f32[4,128]{1,0:T(4,128)S(1)} collective-permute-done((f32[4,128]{1,0:T(4,128)S(1)}, f32[4,128]{1,0:T(4,128)S(1)}, u32[]{:S(2)}, u32[]{:S(2)}) %collective-permute-start.3) | collective-permute-done | bytes 2080 | tf_op jit(solution)/shard_map/ppermute | solution.py:420
  24.6 0.4 edges.1.edge
  25.0 1.6 %scatter.1 = (f32[72,8,128]{2,1,0:T(8,128)S(1)}, f32[72,8,128]{2,1,0:T(8,128)S(1)}, f32[72,8,128]{2,1,0:T(8,128)S(1)}, f32[72,8,128]{2,1,0:T(8,128)S(1)}) custom-call(s32[4,16]{1,0:T(4,128)S(1)} %copy-done.4, s32[4,16]{1,0:T(4,128)S(1)} %collective-permute-done.rows_other, f32[64,8,128]{2,1,0:T(8,128)S(1)} %get-tuple-element.13.own, ...), custom_call_target="tpu_custom_call" | custom-call | flops 1000000 | bytes 1000000 | tf_op jit(solution)/shard_map/scatter/pallas_call | solution.py:296
  26.5 0.1 collective-permute-start.4
  26.6 0.1 collective-permute-start.5
  26.7 2.7 %collective-permute-start.6 = (f32[72,8,128]{2,1,0:T(8,128)S(1)}, f32[72,8,128]{2,1,0:T(8,128)S(1)}, u32[]{:S(2)}, u32[]{:S(2)}) collective-permute-start(f32[72,8,128]{2,1,0:T(8,128)S(1)} %get-tuple-element.18), channel_id=1, source_target_pairs={{0,192},{1,49},{2,194},{3,51},{4,196},{5,53},{6,198},{7,55},{8,200... | collective-permute-start | bytes 884744 | tf_op jit(solution)/shard_map/ppermute | solution.py:426
  29.4 4.6 %collective-permute-done.4 = f32[72,8,128]{2,1,0:T(8,128)S(1)} collective-permute-done((f32[72,8,128]{2,1,0:T(8,128)S(1)}, f32[72,8,128]{2,1,0:T(8,128)S(1)}, u32[]{:S(2)}, u32[]{:S(2)}) %collective-permute-start.4) | collective-permute-done | bytes 294944 | tf_op jit(solution)/shard_map/ppermute | solution.py:426
  34.0 2.9 %collective-permute-done.5 = f32[72,8,128]{2,1,0:T(8,128)S(1)} collective-permute-done((f32[72,8,128]{2,1,0:T(8,128)S(1)}, f32[72,8,128]{2,1,0:T(8,128)S(1)}, u32[]{:S(2)}, u32[]{:S(2)}) %collective-permute-start.5) | collective-permute-done | bytes 294944 | tf_op jit(solution)/shard_map/ppermute | solution.py:426
  37.1 0.6 %collective-permute-start.9 = (f32[18,8,128]{2,1,0:T(8,128)S(1)}, f32[18,8,128]{2,1,0:T(8,128)S(1)}, u32[]{:S(2)}, u32[]{:S(2)}) collective-permute-start(f32[18,8,128]{2,1,0:T(8,128)S(1)} %get-tuple-element.21), channel_id=1, source_target_pairs={{0,48},{1,193},{2,50},{3,195},{4,52},{5,197},{6,54},{7,199},{8,56}... | collective-permute-start | bytes 221192 | tf_op jit(solution)/shard_map/ppermute | solution.py:430
  37.7 0.9 %collective-permute-start.8 = (f32[18,8,128]{2,1,0:T(8,128)S(1)}, f32[18,8,128]{2,1,0:T(8,128)S(1)}, u32[]{:S(2)}, u32[]{:S(2)}) collective-permute-start(f32[18,8,128]{2,1,0:T(8,128)S(1)} %get-tuple-element.22), channel_id=1, source_target_pairs={{0,16},{1,65},{2,18},{3,67},{4,20},{5,69},{6,22},{7,71},{8,24},{9,... | collective-permute-start | bytes 221192 | tf_op jit(solution)/shard_map/ppermute | solution.py:430
  38.6 0.4 collective-permute-start.7
  39.0 1.3 %collective-permute-done.9.part3 = f32[18,8,128]{2,1,0:T(8,128)S(1)} collective-permute-done((f32[18,8,128]{2,1,0:T(8,128)S(1)}, f32[18,8,128]{2,1,0:T(8,128)S(1)}, u32[]{:S(2)}, u32[]{:S(2)}) %collective-permute-start.9) | collective-permute-done | bytes 73760 | tf_op jit(solution)/shard_map/ppermute | solution.py:430
  40.3 1.8 %collective-permute-done.8.part2 = f32[18,8,128]{2,1,0:T(8,128)S(1)} collective-permute-done((f32[18,8,128]{2,1,0:T(8,128)S(1)}, f32[18,8,128]{2,1,0:T(8,128)S(1)}, u32[]{:S(2)}, u32[]{:S(2)}) %collective-permute-start.8) | collective-permute-done | bytes 73760 | tf_op jit(solution)/shard_map/ppermute | solution.py:430
  42.1 1.2 %collective-permute-done.7.part1 = f32[18,8,128]{2,1,0:T(8,128)S(1)} collective-permute-done((f32[18,8,128]{2,1,0:T(8,128)S(1)}, f32[18,8,128]{2,1,0:T(8,128)S(1)}, u32[]{:S(2)}, u32[]{:S(2)}) %collective-permute-start.7) | collective-permute-done | bytes 73760 | tf_op jit(solution)/shard_map/ppermute | solution.py:430
  43.4 0.1 collective-permute-start.10
  43.5 3.1 %collective-permute-done.10 = f32[4,4,8,128]{3,2,1,0:T(8,128)S(1)} collective-permute-done((f32[4,4,8,128]{3,2,1,0:T(8,128)S(1)}, f32[4,4,8,128]{3,2,1,0:T(8,128)S(1)}, u32[]{:S(2)}, u32[]{:S(2)}) %collective-permute-start.10) | collective-permute-done | bytes 65568 | tf_op jit(solution)/shard_map/ppermute | solution.py:432
  46.6 2.0 %collective-permute-start.11 = (f32[4,8,128]{2,1,0:T(8,128)S(1)}, f32[4,8,128]{2,1,0:T(8,128)S(1)}, u32[]{:S(2)}, u32[]{:S(2)}) collective-permute-start(f32[4,8,128]{2,1,0:T(8,128)S(1)} %get-tuple-element.25), channel_id=1, source_target_pairs={{0,8},{2,10},{4,12},{6,14},{8,0},{10,2},{12,4},{14,6},{1,9},{3,11}... | collective-permute-start | bytes 49160 | tf_op jit(solution)/shard_map/ppermute | solution.py:435
  48.5 1.5 %collective-permute-start.13 = (f32[4,8,128]{2,1,0:T(8,128)S(1)}, f32[4,8,128]{2,1,0:T(8,128)S(1)}, u32[]{:S(2)}, u32[]{:S(2)}) collective-permute-start(f32[4,8,128]{2,1,0:T(8,128)S(1)} %get-tuple-element.26), channel_id=1, source_target_pairs={{0,12},{2,14},{4,0},{6,2},{8,4},{10,6},{12,8},{14,10},{1,13},{3,15... | collective-permute-start | bytes 49160 | tf_op jit(solution)/shard_map/ppermute | solution.py:435
  50.1 2.0 %collective-permute-start.12 = (f32[4,8,128]{2,1,0:T(8,128)S(1)}, f32[4,8,128]{2,1,0:T(8,128)S(1)}, u32[]{:S(2)}, u32[]{:S(2)}) collective-permute-start(f32[4,8,128]{2,1,0:T(8,128)S(1)} %get-tuple-element.27), channel_id=1, source_target_pairs={{0,4},{2,6},{4,8},{6,10},{8,12},{10,14},{12,0},{14,2},{1,5},{3,7},... | collective-permute-start | bytes 49160 | tf_op jit(solution)/shard_map/ppermute | solution.py:435
  52.1 1.3 %collective-permute-done.11 = f32[4,8,128]{2,1,0:T(8,128)S(1)} collective-permute-done((f32[4,8,128]{2,1,0:T(8,128)S(1)}, f32[4,8,128]{2,1,0:T(8,128)S(1)}, u32[]{:S(2)}, u32[]{:S(2)}) %collective-permute-start.11) | collective-permute-done | bytes 16416 | tf_op jit(solution)/shard_map/ppermute | solution.py:435
  53.4 1.4 %collective-permute-done.12 = f32[4,8,128]{2,1,0:T(8,128)S(1)} collective-permute-done((f32[4,8,128]{2,1,0:T(8,128)S(1)}, f32[4,8,128]{2,1,0:T(8,128)S(1)}, u32[]{:S(2)}, u32[]{:S(2)}) %collective-permute-start.12) | collective-permute-done | bytes 16416 | tf_op jit(solution)/shard_map/ppermute | solution.py:435
  54.8 5.2 %collective-permute-start.14 = (f32[32,128]{1,0:T(8,128)S(1)}, f32[32,128]{1,0:T(8,128)S(1)}, u32[]{:S(2)}, u32[]{:S(2)}) collective-permute-start(f32[32,128]{1,0:T(8,128)S(1)} %fusion.3.mine), channel_id=1, source_target_pairs={{0,1},{1,0},{2,3},{3,2},{4,5},{5,4},{6,7},{7,6},{8,9},{9,8},{10,11... | collective-permute-start | bytes 49160 | tf_op jit(solution)/shard_map/ppermute | solution.py:437
  60.0 0.8 %collective-permute-done.14.peer = f32[32,128]{1,0:T(8,128)S(1)} collective-permute-done((f32[32,128]{1,0:T(8,128)S(1)}, f32[32,128]{1,0:T(8,128)S(1)}, u32[]{:S(2)}, u32[]{:S(2)}) %collective-permute-start.14) | collective-permute-done | bytes 16416 | tf_op jit(solution)/shard_map/ppermute | solution.py:437
  60.8 1.1 %inverse.1 = f32[4,1024]{1,0:T(4,128)} custom-call(f32[4,1024]{1,0:T(4,128)S(1)} %copy-done.2, f32[32,128]{1,0:T(8,128)S(1)} %fusion.3.mine, f32[32,128]{1,0:T(8,128)S(1)} %collective-permute-done.14.peer), custom_call_target="tpu_custom_call" | custom-call | flops 1000000 | bytes 100000 | tf_op jit(solution)/shard_map/inverse/pallas_call | solution.py:399
  (21 shorter events, 0.2 us)
Async XLA Ops:
  0.0 3.4 %copy-start = (bf16[4,16,256,256]{3,2,1,0:T(8,128)(2,1)S(1)}, bf16[4,16,256,256]{3,2,1,0:T(8,128)(2,1)}, u32[]{:S(2)}) copy-start(bf16[4,16,256,256]{3,2,1,0:T(8,128)(2,1)} %param.6) | copy-start | bytes 25165828
  3.4 0.7 %copy-start.1 = (f32[4,1024]{1,0:T(4,128)S(1)}, f32[4,1024]{1,0:T(4,128)}, u32[]{:S(2)}) copy-start(f32[4,1024]{1,0:T(4,128)} %density.5) | copy-start | bytes 49156
  4.1 0.7 %copy-start.5 = (s32[4]{0:T(128)S(1)}, s32[4]{0:T(128)}, u32[]{:S(2)}) copy-start(s32[4]{0:T(128)} %counts.1) | copy-start | bytes 52
  4.8 8.5 %copy-start.2 = (f32[4,1024]{1,0:T(4,128)S(1)}, f32[4,1024]{1,0:T(4,128)}, u32[]{:S(2)}) copy-start(f32[4,1024]{1,0:T(4,128)} %density.5) | copy-start | bytes 49156
  4.8 19.0 %copy-start.4 = (s32[4,16]{1,0:T(4,128)S(1)}, s32[4,16]{1,0:T(4,128)}, u32[]{:S(2)}) copy-start(s32[4,16]{1,0:T(4,128)} %rows_own.1) | copy-start | bytes 772
  4.8 19.8 %copy-start.3 = (f32[128,128]{1,0:T(8,128)S(1)}, f32[128,128]{1,0:T(8,128)}, u32[]{:S(2)}) copy-start(f32[128,128]{1,0:T(8,128)} %constant.8.clone.table) | copy-start | bytes 196612
  10.0 15.0 %collective-permute-start.1 = (f32[64,8,128]{2,1,0:T(8,128)S(1)}, f32[64,8,128]{2,1,0:T(8,128)S(1)}, u32[]{:S(2)}, u32[]{:S(2)}) collective-permute-start(f32[64,8,128]{2,1,0:T(8,128)S(1)} %get-tuple-element.14), channel_id=1, source_target_pairs={{0,1},{1,0},{2,3},{3,2},{4,5},{5,4},{6,7},{7,6},{8,9},{9,8},{10,11... | collective-permute-start | bytes 786440 | tf_op jit(solution)/shard_map/ppermute | solution.py:419
  13.3 9.2 %collective-permute-start.2 = (f32[4,128]{1,0:T(4,128)S(1)}, f32[4,128]{1,0:T(4,128)S(1)}, u32[]{:S(2)}, u32[]{:S(2)}) collective-permute-start(f32[4,128]{1,0:T(4,128)S(1)} %slice_select_fusion), channel_id=1, source_target_pairs={{0,2},{1,255},{2,4},{3,1},{4,6},{5,3},{6,8},{7,5},{8,10},{9,7},{10... | collective-permute-start | bytes 6152 | tf_op jit(solution)/shard_map/ppermute | solution.py:416
  22.6 2.0 %collective-permute-start.3 = (f32[4,128]{1,0:T(4,128)S(1)}, f32[4,128]{1,0:T(4,128)S(1)}, u32[]{:S(2)}, u32[]{:S(2)}) collective-permute-start(f32[4,128]{1,0:T(4,128)S(1)} %collective-permute-done.2.mine), channel_id=1, source_target_pairs={{0,1},{1,0},{2,3},{3,2},{4,5},{5,4},{6,7},{7,6},{8,9},{9,8},{10,11... | collective-permute-start | bytes 6152 | tf_op jit(solution)/shard_map/ppermute | solution.py:420
  23.8 1.2 %collective-permute-start = (s32[4,16]{1,0:T(4,128)S(1)}, s32[4,16]{1,0:T(4,128)S(1)}, u32[]{:S(2)}, u32[]{:S(2)}) collective-permute-start(s32[4,16]{1,0:T(4,128)S(1)} %copy-done.4), channel_id=1, source_target_pairs={{0,1},{1,0},{2,3},{3,2},{4,5},{5,4},{6,7},{7,6},{8,9},{9,8},{10,11... | collective-permute-start | bytes 776 | tf_op jit(solution)/shard_map/ppermute | solution.py:417
  26.5 7.5 %collective-permute-start.4 = (f32[72,8,128]{2,1,0:T(8,128)S(1)}, f32[72,8,128]{2,1,0:T(8,128)S(1)}, u32[]{:S(2)}, u32[]{:S(2)}) collective-permute-start(f32[72,8,128]{2,1,0:T(8,128)S(1)} %get-tuple-element.16), channel_id=1, source_target_pairs={{0,128},{1,33},{2,130},{3,35},{4,132},{5,37},{6,134},{7,39},{8,136... | collective-permute-start | bytes 884744 | tf_op jit(solution)/shard_map/ppermute | solution.py:426
  26.6 10.3 %collective-permute-start.5 = (f32[72,8,128]{2,1,0:T(8,128)S(1)}, f32[72,8,128]{2,1,0:T(8,128)S(1)}, u32[]{:S(2)}, u32[]{:S(2)}) collective-permute-start(f32[72,8,128]{2,1,0:T(8,128)S(1)} %get-tuple-element.17), channel_id=1, source_target_pairs={{0,64},{1,17},{2,66},{3,19},{4,68},{5,21},{6,70},{7,23},{8,72},{9,... | collective-permute-start | bytes 884744 | tf_op jit(solution)/shard_map/ppermute | solution.py:426
  26.7 10.2 %collective-permute-start.6 = (f32[72,8,128]{2,1,0:T(8,128)S(1)}, f32[72,8,128]{2,1,0:T(8,128)S(1)}, u32[]{:S(2)}, u32[]{:S(2)}) collective-permute-start(f32[72,8,128]{2,1,0:T(8,128)S(1)} %get-tuple-element.18), channel_id=1, source_target_pairs={{0,192},{1,49},{2,194},{3,51},{4,196},{5,53},{6,198},{7,55},{8,200... | collective-permute-start | bytes 884744 | tf_op jit(solution)/shard_map/ppermute | solution.py:426
  37.1 3.3 %collective-permute-start.9 = (f32[18,8,128]{2,1,0:T(8,128)S(1)}, f32[18,8,128]{2,1,0:T(8,128)S(1)}, u32[]{:S(2)}, u32[]{:S(2)}) collective-permute-start(f32[18,8,128]{2,1,0:T(8,128)S(1)} %get-tuple-element.21), channel_id=1, source_target_pairs={{0,48},{1,193},{2,50},{3,195},{4,52},{5,197},{6,54},{7,199},{8,56}... | collective-permute-start | bytes 221192 | tf_op jit(solution)/shard_map/ppermute | solution.py:430
  37.7 4.4 %collective-permute-start.8 = (f32[18,8,128]{2,1,0:T(8,128)S(1)}, f32[18,8,128]{2,1,0:T(8,128)S(1)}, u32[]{:S(2)}, u32[]{:S(2)}) collective-permute-start(f32[18,8,128]{2,1,0:T(8,128)S(1)} %get-tuple-element.22), channel_id=1, source_target_pairs={{0,16},{1,65},{2,18},{3,67},{4,20},{5,69},{6,22},{7,71},{8,24},{9,... | collective-permute-start | bytes 221192 | tf_op jit(solution)/shard_map/ppermute | solution.py:430
  38.6 4.7 %collective-permute-start.7 = (f32[18,8,128]{2,1,0:T(8,128)S(1)}, f32[18,8,128]{2,1,0:T(8,128)S(1)}, u32[]{:S(2)}, u32[]{:S(2)}) collective-permute-start(f32[18,8,128]{2,1,0:T(8,128)S(1)} %get-tuple-element.23), channel_id=1, source_target_pairs={{0,32},{1,129},{2,34},{3,131},{4,36},{5,133},{6,38},{7,135},{8,40}... | collective-permute-start | bytes 221192 | tf_op jit(solution)/shard_map/ppermute | solution.py:430
  43.4 3.2 %collective-permute-start.10 = (f32[4,4,8,128]{3,2,1,0:T(8,128)S(1)}, f32[4,4,8,128]{3,2,1,0:T(8,128)S(1)}, u32[]{:S(2)}, u32[]{:S(2)}) collective-permute-start(f32[4,4,8,128]{3,2,1,0:T(8,128)S(1)} %get-tuple-element.20), channel_id=1, source_target_pairs={{0,2},{2,0},{4,6},{6,4},{8,10},{10,8},{12,14},{14,12},{1,3},{3,1},... | collective-permute-start | bytes 196616 | tf_op jit(solution)/shard_map/ppermute | solution.py:432
  46.6 6.8 %collective-permute-start.11 = (f32[4,8,128]{2,1,0:T(8,128)S(1)}, f32[4,8,128]{2,1,0:T(8,128)S(1)}, u32[]{:S(2)}, u32[]{:S(2)}) collective-permute-start(f32[4,8,128]{2,1,0:T(8,128)S(1)} %get-tuple-element.25), channel_id=1, source_target_pairs={{0,8},{2,10},{4,12},{6,14},{8,0},{10,2},{12,4},{14,6},{1,9},{3,11}... | collective-permute-start | bytes 49160 | tf_op jit(solution)/shard_map/ppermute | solution.py:435
  48.5 4.8 %collective-permute-start.13 = (f32[4,8,128]{2,1,0:T(8,128)S(1)}, f32[4,8,128]{2,1,0:T(8,128)S(1)}, u32[]{:S(2)}, u32[]{:S(2)}) collective-permute-start(f32[4,8,128]{2,1,0:T(8,128)S(1)} %get-tuple-element.26), channel_id=1, source_target_pairs={{0,12},{2,14},{4,0},{6,2},{8,4},{10,6},{12,8},{14,10},{1,13},{3,15... | collective-permute-start | bytes 49160 | tf_op jit(solution)/shard_map/ppermute | solution.py:435
  50.1 4.7 %collective-permute-start.12 = (f32[4,8,128]{2,1,0:T(8,128)S(1)}, f32[4,8,128]{2,1,0:T(8,128)S(1)}, u32[]{:S(2)}, u32[]{:S(2)}) collective-permute-start(f32[4,8,128]{2,1,0:T(8,128)S(1)} %get-tuple-element.27), channel_id=1, source_target_pairs={{0,4},{2,6},{4,8},{6,10},{8,12},{10,14},{12,0},{14,2},{1,5},{3,7},... | collective-permute-start | bytes 49160 | tf_op jit(solution)/shard_map/ppermute | solution.py:435
  54.8 6.0 %collective-permute-start.14 = (f32[32,128]{1,0:T(8,128)S(1)}, f32[32,128]{1,0:T(8,128)S(1)}, u32[]{:S(2)}, u32[]{:S(2)}) collective-permute-start(f32[32,128]{1,0:T(8,128)S(1)} %fusion.3.mine), channel_id=1, source_target_pairs={{0,1},{1,0},{2,3},{3,2},{4,5},{5,4},{6,7},{7,6},{8,9},{9,8},{10,11... | collective-permute-start | bytes 49160 | tf_op jit(solution)/shard_map/ppermute | solution.py:437

commit v3 on v2

--- a/solution.py
+++ b/solution.py
@@ -6,12 +6,13 @@
 from jax.experimental.pallas import tpu as pltpu
 from jax.sharding import Mesh, PartitionSpec as P
 
+
 LEVELS = 3
 NX, NY, NZ, NC = 4, 4, 8, 2
 PATCH = ("x", "y", "z")
 ALL = ("x", "y", "z", "c")
 OWNERS = NX * NY * NZ
-TILES = 2 * NZ + 2
+TILES = 2 * NZ + 1
 COLS, SLOTS, BS = 4, 16, 256
 HELD = COLS * SLOTS
 LEN = COLS * BS
@@ -29,6 +30,38 @@
         pairs.append((p * NC, ((p + 1) % OWNERS) * NC))
         pairs.append((p * NC + 1, ((p - 1) % OWNERS) * NC + 1))
     return pairs
+
+
+def stage_kernel(density, staged, edge):
+    core = lax.axis_index("c")
+    value = density[...]
+    staged[...] = value
+    edge[...] = jnp.where(core == 0, value[:, LEN - 128 :], value[:, :128])
+
+
+def stage(density):
+    vmem = pl.BlockSpec(memory_space=pltpu.VMEM)
+    return pl.pallas_call(
+        stage_kernel,
+        in_specs=[vmem],
+        out_specs=[vmem, vmem],
+        out_shape=[
+            jax.ShapeDtypeStruct(density.shape, jnp.float32),
+            jax.ShapeDtypeStruct((4, 128), jnp.float32),
+        ],
+        compiler_params=pltpu.CompilerParams(vmem_limit_bytes=SMALL),
+        name="stage",
+    )(density)
+
+
+def pack_edges(after, before):
+    lane = lax.broadcasted_iota(jnp.int32, (8, 128), 1)
+    tiles = [jnp.where(lane < 64, high, low) for high, low in zip(after, before)]
+    return jnp.where((lane >= 16) & (lane < 48), pltpu.roll(tiles[1], 32, 1), tiles[0])
+
+
+def unpack_edges(tile):
+    return tile, pltpu.roll(tile, 96, 1)
 
 
 def line_pairs(shift, swap):
@@ -77,15 +110,16 @@
     return [lax.axis_index(axis) for axis in ALL]
 
 
-def terms_kernel(counts, density, values, own, send, wide, xt, d1, s1, d2, s2, d3, vec, acc, held, sems):
+CHUNKS = {0: 4, 4: 12, 16: 16, 32: 16, 48: 16}
+
+
+def terms_kernel(density, values, own, send, wide, xt, d1, s1, d2, s2, d3, vec, acc, held, sems):
     core = lax.axis_index("c")
-    parts = 8
-    size = HELD // parts
-    copies = [
-        pltpu.make_async_copy(values.at[pl.ds(i * size, size)], held.at[pl.ds(i * size, size)], sems.at[i])
-        for i in range(parts)
-    ]
-    for copy in copies:
+    copies = {
+        at: pltpu.make_async_copy(values.at[pl.ds(at, size)], held.at[pl.ds(at, size)], sems.at[i])
+        for i, (at, size) in enumerate(CHUNKS.items())
+    }
+    for copy in copies.values():
         copy.start()
     wide[0:4, :] = density[...]
     wide[4:8, :] = density[...]
@@ -154,13 +188,11 @@
     whose = lax.broadcasted_iota(jnp.int32, (1, 128), 1) >> 3
     for column in range(COLS):
         vector = vec[pl.ds(column * BS, BS), :].astype(jnp.bfloat16)
-        total = None
         for slot in range(SLOTS):
             index = column * SLOTS + slot
-            if index % size == 0:
-                copies[index // size].wait()
-            live = core * SLOTS + slot < counts[column]
-            mask = (whose == jnp.where(live, slot, -1)).astype(jnp.float32).astype(jnp.bfloat16)
+            if index in copies:
+                copies[index].wait()
+            mask = (whose == slot).astype(jnp.float32).astype(jnp.bfloat16)
             part = jnp.dot(held[index], vector * mask, preferred_element_type=jnp.float32)
             if slot == 0:
                 acc[...] = part
@@ -174,14 +206,13 @@
         send[at] = jnp.where(core == 0, high, low)
 
 
-def terms(counts, density, values):
-    smem = pl.BlockSpec(memory_space=pltpu.SMEM)
+def terms(density, values):
     vmem = pl.BlockSpec(memory_space=pltpu.VMEM)
     block = jax.ShapeDtypeStruct((HELD, 8, 128), jnp.float32)
     f32 = jnp.float32
     return pl.pallas_call(
         terms_kernel,
-        in_specs=[smem, vmem, pl.BlockSpec(memory_space=pltpu.HBM)],
+        in_specs=[vmem, pl.BlockSpec(memory_space=pltpu.HBM)],
         out_specs=[vmem, vmem],
         out_shape=[block, block],
         scratch_shapes=[
@@ -195,14 +226,14 @@
             pltpu.VMEM((LEN, 128), f32),
             pltpu.VMEM((BS, 128), f32),
             pltpu.VMEM((HELD, BS, BS), jnp.bfloat16),
-            pltpu.SemaphoreType.DMA((8,)),
+            pltpu.SemaphoreType.DMA((len(CHUNKS),)),
         ],
-        compiler_params=pltpu.CompilerParams(vmem_limit_bytes=16 * 1024 * 1024),
+        compiler_params=pltpu.CompilerParams(vmem_limit_bytes=50 * 1024 * 1024),
         cost_estimate=pl.CostEstimate(
             flops=2 * HELD * BS * BS * 128, bytes_accessed=2 * HELD * BS * BS, transcendentals=0
         ),
         name="terms",
-    )(counts, density, values)
+    )(density, values)
 
 
 def edges_kernel(density, mine, other, table, out):
@@ -245,8 +276,33 @@
     )(density, mine, other, table)
 
 
-def scatter_kernel(rows_own, rows_other, own, other, edge, out0, out1, out2, out3, dense, staged, base):
+def scatter_kernel(
+    counts_ref,
+    rows_ref,
+    rows_other_ref,
+    own,
+    other,
+    edge,
+    out0,
+    out1,
+    out2,
+    out3,
+    dense,
+    staged,
+    base,
+    counts,
+    rows_own,
+    rows_other,
+    sems,
+):
     x, y, _, core = coordinates()
+    copies = [
+        pltpu.make_async_copy(rows_ref, rows_own, sems.at[0]),
+        pltpu.make_async_copy(rows_other_ref, rows_other, sems.at[1]),
+        pltpu.make_async_copy(counts_ref, counts, sems.at[2]),
+    ]
+    for copy in copies:
+        copy.start()
 
     def relative(column_x, column_y):
         dx, dy = (column_x - x) & 3, (column_y - y) & 3
@@ -256,6 +312,8 @@
         base[column] = relative(column >> 2, column & 3) * TILES
     dense[...] = jnp.zeros_like(dense)
     sub = lax.broadcasted_iota(jnp.int32, (SLOTS, 8, 128), 1)
+    number = lax.broadcasted_iota(jnp.int32, (SLOTS, 8, 128), 0)
+    copies[2].wait()
     which = ((0, 1, 2), (3, 4), (), (5,))
     for side, source in enumerate((own, other)):
         for column in range(COLS):
@@ -263,65 +321,74 @@
             total = tile
             for place, index in enumerate(which[column]):
                 total = total + tile[:, 4 + place : 5 + place, :] * edge[index][None]
-            total = jnp.where(sub < 4, total, 0.0)
+            first_slot = (core if side == 0 else 1 - core) * SLOTS
+            live = (sub < 4) & (number < counts[column] - first_slot)
+            total = jnp.where(live, total, 0.0)
             at = pl.ds((side * COLS + column) * SLOTS, SLOTS)
             staged[0, at] = total
             staged[1, at] = pltpu.roll(total, 4, 1)
+    for copy in copies[:2]:
+        copy.wait()
     for side, rows in enumerate((rows_own, rows_other)):
         for column in range(COLS):
             for slot in range(SLOTS):
-                number = rows[column, slot]
-                spot = base[number >> 5] + ((number >> 1) & 15)
-                value = staged[number & 1, (side * COLS + column) * SLOTS + slot]
+                row = rows[column, slot]
+                spot = base[row >> 5] + ((row >> 1) & 15)
+                value = staged[row & 1, (side * COLS + column) * SLOTS + slot]
                 dense[spot] = dense[spot] + value
-    lane = lax.broadcasted_iota(jnp.int32, (2, 8, 128), 2)
-    for first in range(4):
-        for second in range(4):
-            here = (first * 4 + second) * TILES
-            cx = (jnp.where(core == 0, first, second) + x) & 3
-            cy = (jnp.where(core == 0, second, first) + y) & 3
-            column = cx * 4 + cy
-            high = jnp.where(column == 15, 0.0, dense[pl.ds(base[(column + 1) & 15], 2)])
-            low = jnp.where(column == 0, 0.0, dense[pl.ds(base[(column + 15) & 15] + 14, 2)])
-            dense[pl.ds(here + 2 * NZ, 2)] = jnp.where(lane < 64, high, low)
+    packed = []
+    for column in range(16):
+        after, before = [], []
+        for tile in range(2):
+            if column == 15:
+                after.append(jnp.zeros((8, 128), jnp.float32))
+            else:
+                after.append(dense[base[column + 1] + tile])
+            if column == 0:
+                before.append(jnp.zeros((8, 128), jnp.float32))
+            else:
+                before.append(dense[base[column - 1] + 2 * NZ - 2 + tile])
+        packed.append(pack_edges(after, before))
+    for column in range(16):
+        dense[base[column] + 2 * NZ] = packed[column]
     size = 4 * TILES
     for index, out in enumerate((out0, out1, out2, out3)):
         out[...] = dense[pl.ds(index * size, size)]
 
 
-def scatter(rows_own, rows_other, own, other, edge):
+def scatter(counts, rows_own, rows_other, own, other, edge):
     size = 4 * TILES
-    smem = pl.BlockSpec(memory_space=pltpu.SMEM)
+    anywhere = pl.BlockSpec(memory_space=pl.ANY)
     vmem = pl.BlockSpec(memory_space=pltpu.VMEM)
     return pl.pallas_call(
         scatter_kernel,
-        in_specs=[smem] * 2 + [vmem] * 3,
+        in_specs=[anywhere] * 3 + [vmem] * 3,
         out_specs=[vmem] * 4,
         out_shape=[jax.ShapeDtypeStruct((size, 8, 128), jnp.float32)] * 4,
         scratch_shapes=[
             pltpu.VMEM((4 * size, 8, 128), jnp.float32),
             pltpu.VMEM((2, 2 * HELD, 8, 128), jnp.float32),
             pltpu.SMEM((16,), jnp.int32),
+            pltpu.SMEM((COLS,), jnp.int32),
+            pltpu.SMEM((COLS, SLOTS), jnp.int32),
+            pltpu.SMEM((COLS, SLOTS), jnp.int32),
+            pltpu.SemaphoreType.DMA((3,)),
         ],
         compiler_params=pltpu.CompilerParams(vmem_limit_bytes=2 * SMALL),
         cost_estimate=pl.CostEstimate(flops=10**6, bytes_accessed=10**6, transcendentals=0),
         name="scatter",
-    )(rows_own, rows_other, own, other, edge)
-
-
-def messages_kernel(part0, part1, part2, part3, keep, send, total):
-    z = lax.axis_index("z")
-    total[...] = (part0[...] + part1[...]) + (part2[...] + part3[...])
-    lane = lax.broadcasted_iota(jnp.int32, (2, 8, 128), 2)
-    for out, parity in ((keep, z & 1), (send, 1 - (z & 1))):
-        for index in range(4):
-            owner = (((z >> 1) + index) & 3) * 2 + parity
-            after = jnp.where(owner == NZ - 1, NZ, owner + 1)
-            before = jnp.where(owner == 0, NZ, owner - 1)
-            out[index, 0:2] = total[pl.ds(owner * 2, 2)]
-            out[index, 2:4] = jnp.where(
-                lane < 64, total[pl.ds(after * 2, 2)], total[pl.ds(before * 2, 2)]
-            )
+    )(counts, rows_own, rows_other, own, other, edge)
+
+
+def messages_kernel(part0, part1, part2, part3, out, total):
+    total[0:TILES] = (part0[...] + part1[...]) + (part2[...] + part3[...])
+    ends = unpack_edges(total[2 * NZ])
+    for owner in range(NZ):
+        here = 2 * owner
+        out[owner, 0:2] = total[here : here + 2]
+        after = ends if owner == NZ - 1 else (total[here + 2], total[here + 3])
+        before = ends if owner == 0 else (total[here - 2], total[here - 1])
+        out[owner, 2] = pack_edges(after, before)
 
 
 def messages(parts):
@@ -329,8 +396,8 @@
     return pl.pallas_call(
         messages_kernel,
         in_specs=[vmem] * 4,
-        out_specs=[vmem] * 2,
-        out_shape=[jax.ShapeDtypeStruct((4, 4, 8, 128), jnp.float32)] * 2,
+        out_specs=vmem,
+        out_shape=jax.ShapeDtypeStruct((NZ, 3, 8, 128), jnp.float32),
         scratch_shapes=[pltpu.VMEM((TILES, 8, 128), jnp.float32)],
         compiler_params=pltpu.CompilerParams(vmem_limit_bytes=SMALL),
         cost_estimate=pl.CostEstimate(flops=10**5, bytes_accessed=10**5, transcendentals=0),
@@ -342,9 +409,10 @@
     x, y, z, core = coordinates()
     last = ((x * NY + y) * NZ + z) == OWNERS - 1
     inside = jnp.where(last, 0.0, 1.0)
-    first = jnp.where(core == 0, mine[...], peer[...])
-    second = jnp.where(core == 0, peer[...], mine[...])
-    both = jnp.concatenate([first, second, jnp.zeros((64, 128), jnp.float32)], axis=0)
+    rows = []
+    for half in (jnp.where(core == 0, mine[...], peer[...]), jnp.where(core == 0, peer[...], mine[...])):
+        rows += [half[0:16], *unpack_edges(half[16:24])]
+    both = jnp.concatenate(rows + [jnp.zeros((64, 128), jnp.float32)], axis=0)
     turned[...] = both.T
 
     def piece(half, block):
@@ -410,16 +478,15 @@
 
 
 def body(density, block_values, block_rows, block_counts):
-    core = lax.axis_index("c")
     across = [(0, 1), (1, 0)]
-    edge = jnp.where(core == 0, density[:, -128:], density[:, :128])
+    density, edge = stage(density)
     halo = lax.ppermute(edge, ALL, halo_pairs())
     rows_other = lax.ppermute(block_rows, "c", across)
-    own, send = terms(block_counts, density, block_values.reshape(HELD, BS, BS))
+    own, send = terms(density, block_values.reshape(HELD, BS, BS))
     received = lax.ppermute(send, "c", across)
     halo_other = lax.ppermute(halo, "c", across)
     edge_values = edges(density, halo, halo_other, jnp.asarray(edge_table()))
-    parts = scatter(block_rows, rows_other, own, received, edge_values)
+    parts = scatter(block_counts, block_rows, rows_other, own, received, edge_values)
 
     first = parts[0]
     for shift in (2, 1, 3):
@@ -428,12 +495,8 @@
     second = [first[0]]
     for shift in (2, 1, 3):
         second.append(lax.ppermute(first[shift], ALL, line_pairs(shift, True)))
-    keep, away = messages(second)
-    keep = keep + lax.ppermute(away, "z", [(i, i ^ 1) for i in range(NZ)])
-    last = keep[0]
-    for shift in (2, 1, 3):
-        last = last + lax.ppermute(keep[shift], "z", [(i, (i + 2 * shift) % NZ) for i in range(NZ)])
-    last = last.reshape(32, 128)
+    last = lax.all_to_all(messages(second), "z", 0, 0, tiled=True).sum(axis=0)
+    last = last.reshape(24, 128)
     return inverse(density, last, lax.ppermute(last, "c", across))
 
 

time: 62.1 us -> 57 us (0.918)
  blocking collectives: 0 us -> 12.1 us
  starting transfers between devices: 28.6 us -> 21.9 us
  waiting for transfers between devices: 20.1 us -> 13.9 us
  local copies, waits for them, and re-layouts: 4.79 us -> 0.78 us
    all_to_all x0 -> x1, blocking collectives: none -> 12.1 us  [body(): last = lax.all_to_all(messages(second), 'z', 0, 0, tiled=True).sum(axis=0)]
    ppermute x4 -> x0, waiting for transfers between devices: 5.81 us -> none  [the longest x1 3.1 us: body(): keep = keep + lax.ppermute(away, 'z', [(i, i ^ 1) for i in range(NZ)])]
    ppermute x4 -> x0, starting transfers between devices: 5.58 us -> none  [the longest x3 5.48 us: body(): lax.ppermute(keep[shift], 'z', [(i, (i + 2 * shift) % NZ) for i in range(...]
    unnamed x12 -> x8, local copies, waits for them, and re-layouts: 4.76 us -> 0.76 us
    ppermute x1, starting transfers between devices: 5.17 us -> 4.12 us  [body(): return inverse(density, last, lax.ppermute(last, 'c', across))]
    pallas_call x3 -> x4, Pallas kernels: 6.85 us -> 6.34 us  [the longest x1 4.58 us: terms(): pl.pallas_call(terms_kernel, in_specs=[vmem, pl.BlockSpec(memory_space=pl...]
  transfers between devices with their start and end apart: 15 -> 11, of which waited for: 11 -> 8; matrix products, arithmetic and copies ran while one was open for 0% -> 0% of each run, Pallas kernels for 1% -> 1%
where the time goes in v3:
time: 57 us; the launch traced here: 56.8 us
  starting transfers between devices  21.9 us (38%)
  waiting for transfers between devices  13.9 us (24%)
  blocking collectives  12.1 us (21%)
  Pallas kernels  7.93 us (14%)
  local copies, waits for them, and re-layouts  0.78 us (1%)
    all_to_all x1, blocking collectives, body(): last = lax.all_to_all(messages(second), 'z', 0, 0, tiled=True).sum(axis=0)  12.1 us
    ppermute x1, starting transfers between devices, body(): halo = lax.ppermute(edge, ALL, halo_pairs())  8.53 us
    ppermute x3, waiting for transfers between devices, body(): first = first + lax.ppermute(parts[shift], ALL, line_pairs(shift, False))  7.21 us
    pallas_call x1, Pallas kernels, terms(): pl.pallas_call(terms_kernel, in_specs=[vmem, pl.BlockSpec(memory_space=pl...  4.58 us
    ppermute x3, waiting for transfers between devices, body(): second.append(lax.ppermute(first[shift], ALL, line_pairs(shift, True)))  4.25 us
    ppermute x1, starting transfers between devices, body(): return inverse(density, last, lax.ppermute(last, 'c', across))  4.12 us
    ppermute x1, starting transfers between devices, body(): received = lax.ppermute(send, 'c', across)  3.28 us
    ppermute x3, starting transfers between devices, body(): first = first + lax.ppermute(parts[shift], ALL, line_pairs(shift, False))  2.84 us
  transfers between devices with their start and end apart: 11, of which 8 were waited for; matrix products, arithmetic and copies ran while one was open for 0% of the time, Pallas kernels for 1%

profile of v3, /device:TPU:1, one launch (start us, length us, event | category | flops | bytes accessed | tf_op | source)
XLA Modules:
  0.0 56.8 jit_solution(11441789834007861364)
XLA Ops:
  0.0 0.7 %copy-done.1 = f32[4,1024]{1,0:T(4,128)S(1)} copy-done((f32[4,1024]{1,0:T(4,128)S(1)}, f32[4,1024]{1,0:T(4,128)}, u32[]{:S(2)}) %copy-start.1) | copy-done | bytes 16408
  0.8 4.6 %terms.1 = (f32[64,8,128]{2,1,0:T(8,128)S(1)}, f32[64,8,128]{2,1,0:T(8,128)S(1)}) custom-call(f32[4,1024]{1,0:T(4,128)S(1)} %get-tuple-element.13.density, bf16[64,256,256]{2,1,0:T(8,128)(2,1)} %bitcast.4), custom_call_target="tpu_custom_call" | custom-call | flops 1073741824 | bytes 8388608 | tf_op jit(solution)/shard_map/terms/pallas_call | solution.py:213
  5.4 3.3 %collective-permute-start.1 = (f32[64,8,128]{2,1,0:T(8,128)S(1)}, f32[64,8,128]{2,1,0:T(8,128)S(1)}, u32[]{:S(2)}, u32[]{:S(2)}) collective-permute-start(f32[64,8,128]{2,1,0:T(8,128)S(1)} %get-tuple-element.15), channel_id=1, source_target_pairs={{0,1},{1,0},{2,3},{3,2},{4,5},{5,4},{6,7},{7,6},{8,9},{9,8},{10,11... | collective-permute-start | bytes 786440 | tf_op jit(solution)/shard_map/ppermute | solution.py:486
  8.6 8.5 %collective-permute-start.2 = (f32[4,128]{1,0:T(4,128)S(1)}, f32[4,128]{1,0:T(4,128)S(1)}, u32[]{:S(2)}, u32[]{:S(2)}) collective-permute-start(f32[4,128]{1,0:T(4,128)S(1)} %get-tuple-element.16), channel_id=1, source_target_pairs={{0,2},{1,255},{2,4},{3,1},{4,6},{5,3},{6,8},{7,5},{8,10},{9,7},{10... | collective-permute-start | bytes 6152 | tf_op jit(solution)/shard_map/ppermute | solution.py:483
  17.2 0.7 %collective-permute-done.2.mine = f32[4,128]{1,0:T(4,128)S(1)} collective-permute-done((f32[4,128]{1,0:T(4,128)S(1)}, f32[4,128]{1,0:T(4,128)S(1)}, u32[]{:S(2)}, u32[]{:S(2)}) %collective-permute-start.2) | collective-permute-done | bytes 2080 | tf_op jit(solution)/shard_map/ppermute | solution.py:483
  17.9 1.2 %collective-permute-start.3 = (f32[4,128]{1,0:T(4,128)S(1)}, f32[4,128]{1,0:T(4,128)S(1)}, u32[]{:S(2)}, u32[]{:S(2)}) collective-permute-start(f32[4,128]{1,0:T(4,128)S(1)} %collective-permute-done.2.mine), channel_id=1, source_target_pairs={{0,1},{1,0},{2,3},{3,2},{4,5},{5,4},{6,7},{7,6},{8,9},{9,8},{10,11... | collective-permute-start | bytes 6152 | tf_op jit(solution)/shard_map/ppermute | solution.py:487
  19.1 0.0 copy-done.2
  19.1 0.0 collective-permute-start
  19.1 0.8 %collective-permute-done.3.other = f32[4,128]{1,0:T(4,128)S(1)} collective-permute-done((f32[4,128]{1,0:T(4,128)S(1)}, f32[4,128]{1,0:T(4,128)S(1)}, u32[]{:S(2)}, u32[]{:S(2)}) %collective-permute-start.3) | collective-permute-done | bytes 2080 | tf_op jit(solution)/shard_map/ppermute | solution.py:487
  19.9 0.0 copy-done
  19.9 0.4 edges.1.edge
  20.3 0.0 collective-permute-done.rows_other_ref
  20.3 0.0 collective-permute-done.1.other
  20.3 1.6 %scatter.1 = (f32[68,8,128]{2,1,0:T(8,128)S(1)}, f32[68,8,128]{2,1,0:T(8,128)S(1)}, f32[68,8,128]{2,1,0:T(8,128)S(1)}, f32[68,8,128]{2,1,0:T(8,128)S(1)}) custom-call(s32[4]{0:T(128)S(1)} %copy-done.3, s32[4,16]{1,0:T(4,128)S(1)} %copy-done.2, s32[4,16]{1,0:T(4,128)S(1)} %collective-permute-done.rows_other_ref, f32[64,8,128]{2,1,0:T(8,128)S(1)} %get-tuple-element.14.own, ...), custom_call_target="tpu_custom_call" | custom-call | flops 1000000 | bytes 1000000 | tf_op jit(solution)/shard_map/scatter/pallas_call | solution.py:363
  21.9 0.1 collective-permute-start.4
  22.0 0.1 collective-permute-start.5
  22.1 2.7 %collective-permute-start.6 = (f32[68,8,128]{2,1,0:T(8,128)S(1)}, f32[68,8,128]{2,1,0:T(8,128)S(1)}, u32[]{:S(2)}, u32[]{:S(2)}) collective-permute-start(f32[68,8,128]{2,1,0:T(8,128)S(1)} %get-tuple-element.20), channel_id=1, source_target_pairs={{0,192},{1,49},{2,194},{3,51},{4,196},{5,53},{6,198},{7,55},{8,200... | collective-permute-start | bytes 835592 | tf_op jit(solution)/shard_map/ppermute | solution.py:493
  24.8 4.5 %collective-permute-done.4 = f32[68,8,128]{2,1,0:T(8,128)S(1)} collective-permute-done((f32[68,8,128]{2,1,0:T(8,128)S(1)}, f32[68,8,128]{2,1,0:T(8,128)S(1)}, u32[]{:S(2)}, u32[]{:S(2)}) %collective-permute-start.4) | collective-permute-done | bytes 278560 | tf_op jit(solution)/shard_map/ppermute | solution.py:493
  29.3 2.7 %collective-permute-done.5 = f32[68,8,128]{2,1,0:T(8,128)S(1)} collective-permute-done((f32[68,8,128]{2,1,0:T(8,128)S(1)}, f32[68,8,128]{2,1,0:T(8,128)S(1)}, u32[]{:S(2)}, u32[]{:S(2)}) %collective-permute-start.5) | collective-permute-done | bytes 278560 | tf_op jit(solution)/shard_map/ppermute | solution.py:493
  32.0 0.0 collective-permute-done.6
  32.0 0.1 add_add_fusion
  32.1 0.6 %collective-permute-start.9 = (f32[17,8,128]{2,1,0:T(8,128)S(1)}, f32[17,8,128]{2,1,0:T(8,128)S(1)}, u32[]{:S(2)}, u32[]{:S(2)}) collective-permute-start(f32[17,8,128]{2,1,0:T(8,128)S(1)} %get-tuple-element.21), channel_id=1, source_target_pairs={{0,48},{1,193},{2,50},{3,195},{4,52},{5,197},{6,54},{7,199},{8,56}... | collective-permute-start | bytes 208904 | tf_op jit(solution)/shard_map/ppermute | solution.py:497
  32.7 0.9 %collective-permute-start.8 = (f32[17,8,128]{2,1,0:T(8,128)S(1)}, f32[17,8,128]{2,1,0:T(8,128)S(1)}, u32[]{:S(2)}, u32[]{:S(2)}) collective-permute-start(f32[17,8,128]{2,1,0:T(8,128)S(1)} %get-tuple-element.22), channel_id=1, source_target_pairs={{0,16},{1,65},{2,18},{3,67},{4,20},{5,69},{6,22},{7,71},{8,24},{9,... | collective-permute-start | bytes 208904 | tf_op jit(solution)/shard_map/ppermute | solution.py:497
  33.6 0.4 collective-permute-start.7
  34.0 1.3 %collective-permute-done.9.part3 = f32[17,8,128]{2,1,0:T(8,128)S(1)} collective-permute-done((f32[17,8,128]{2,1,0:T(8,128)S(1)}, f32[17,8,128]{2,1,0:T(8,128)S(1)}, u32[]{:S(2)}, u32[]{:S(2)}) %collective-permute-start.9) | collective-permute-done | bytes 69664 | tf_op jit(solution)/shard_map/ppermute | solution.py:497
  35.3 1.8 %collective-permute-done.8.part2 = f32[17,8,128]{2,1,0:T(8,128)S(1)} collective-permute-done((f32[17,8,128]{2,1,0:T(8,128)S(1)}, f32[17,8,128]{2,1,0:T(8,128)S(1)}, u32[]{:S(2)}, u32[]{:S(2)}) %collective-permute-start.8) | collective-permute-done | bytes 69664 | tf_op jit(solution)/shard_map/ppermute | solution.py:497
  37.1 1.2 %collective-permute-done.7.part1 = f32[17,8,128]{2,1,0:T(8,128)S(1)} collective-permute-done((f32[17,8,128]{2,1,0:T(8,128)S(1)}, f32[17,8,128]{2,1,0:T(8,128)S(1)}, u32[]{:S(2)}, u32[]{:S(2)}) %collective-permute-start.7) | collective-permute-done | bytes 69664 | tf_op jit(solution)/shard_map/ppermute | solution.py:497
  38.3 0.1 messages.1
  38.4 12.1 %all_to_all.5 = f32[8,3,8,128]{3,2,1,0:T(8,128)S(1)} all-to-all(f32[8,3,8,128]{3,2,1,0:T(8,128)S(1)} %messages.1), channel_id=1, replica_groups=mesh['x'=4,'y'=4,'z'=8,'c'=2] {'z'}, dimensions={0} | all-to-all | bytes 196608 | tf_op jit(solution)/shard_map/all_to_all | solution.py:498
  50.6 4.1 %collective-permute-start.10 = (f32[24,128]{1,0:T(8,128)S(1)}, f32[24,128]{1,0:T(8,128)S(1)}, u32[]{:S(2)}, u32[]{:S(2)}) collective-permute-start(f32[24,128]{1,0:T(8,128)S(1)} %bitcast.2), channel_id=1, source_target_pairs={{0,1},{1,0},{2,3},{3,2},{4,5},{5,4},{6,7},{7,6},{8,9},{9,8},{10,11... | collective-permute-start | bytes 36872 | tf_op jit(solution)/shard_map/ppermute | solution.py:500
  54.7 0.8 %collective-permute-done.10.peer = f32[24,128]{1,0:T(8,128)S(1)} collective-permute-done((f32[24,128]{1,0:T(8,128)S(1)}, f32[24,128]{1,0:T(8,128)S(1)}, u32[]{:S(2)}, u32[]{:S(2)}) %collective-permute-start.10) | collective-permute-done | bytes 12320 | tf_op jit(solution)/shard_map/ppermute | solution.py:500
  55.5 1.2 %inverse.1 = f32[4,1024]{1,0:T(4,128)} custom-call(f32[4,1024]{1,0:T(4,128)S(1)} %get-tuple-element.13.density, f32[24,128]{1,0:T(8,128)S(1)} %bitcast.3, f32[24,128]{1,0:T(8,128)S(1)} %collective-permute-done.10.peer), custom_call_target="tpu_custom_call" | custom-call | flops 1000000 | bytes 100000 | tf_op jit(solution)/shard_map/inverse/pallas_call | solution.py:467
  (8 shorter events, 0.0 us)
Async XLA Ops:
  0.0 19.9 %copy-start = (f32[128,128]{1,0:T(8,128)S(1)}, f32[128,128]{1,0:T(8,128)}, u32[]{:S(2)}) copy-start(f32[128,128]{1,0:T(8,128)} %constant.4.clone.table) | copy-start | bytes 196612
  0.0 0.7 %copy-start.1 = (f32[4,1024]{1,0:T(4,128)S(1)}, f32[4,1024]{1,0:T(4,128)}, u32[]{:S(2)}) copy-start(f32[4,1024]{1,0:T(4,128)} %density.1) | copy-start | bytes 49156
  0.8 18.3 %copy-start.2 = (s32[4,16]{1,0:T(4,128)S(1)}, s32[4,16]{1,0:T(4,128)}, u32[]{:S(2)}) copy-start(s32[4,16]{1,0:T(4,128)} %rows_ref.1) | copy-start | bytes 772
  0.8 19.6 %copy-start.3 = (s32[4]{0:T(128)S(1)}, s32[4]{0:T(128)}, u32[]{:S(2)}) copy-start(s32[4]{0:T(128)} %counts_ref.1) | copy-start | bytes 52
  5.4 14.9 %collective-permute-start.1 = (f32[64,8,128]{2,1,0:T(8,128)S(1)}, f32[64,8,128]{2,1,0:T(8,128)S(1)}, u32[]{:S(2)}, u32[]{:S(2)}) collective-permute-start(f32[64,8,128]{2,1,0:T(8,128)S(1)} %get-tuple-element.15), channel_id=1, source_target_pairs={{0,1},{1,0},{2,3},{3,2},{4,5},{5,4},{6,7},{7,6},{8,9},{9,8},{10,11... | collective-permute-start | bytes 786440 | tf_op jit(solution)/shard_map/ppermute | solution.py:486
  8.6 9.3 %collective-permute-start.2 = (f32[4,128]{1,0:T(4,128)S(1)}, f32[4,128]{1,0:T(4,128)S(1)}, u32[]{:S(2)}, u32[]{:S(2)}) collective-permute-start(f32[4,128]{1,0:T(4,128)S(1)} %get-tuple-element.16), channel_id=1, source_target_pairs={{0,2},{1,255},{2,4},{3,1},{4,6},{5,3},{6,8},{7,5},{8,10},{9,7},{10... | collective-permute-start | bytes 6152 | tf_op jit(solution)/shard_map/ppermute | solution.py:483
  17.9 2.0 %collective-permute-start.3 = (f32[4,128]{1,0:T(4,128)S(1)}, f32[4,128]{1,0:T(4,128)S(1)}, u32[]{:S(2)}, u32[]{:S(2)}) collective-permute-start(f32[4,128]{1,0:T(4,128)S(1)} %collective-permute-done.2.mine), channel_id=1, source_target_pairs={{0,1},{1,0},{2,3},{3,2},{4,5},{5,4},{6,7},{7,6},{8,9},{9,8},{10,11... | collective-permute-start | bytes 6152 | tf_op jit(solution)/shard_map/ppermute | solution.py:487
  19.1 1.2 %collective-permute-start = (s32[4,16]{1,0:T(4,128)S(1)}, s32[4,16]{1,0:T(4,128)S(1)}, u32[]{:S(2)}, u32[]{:S(2)}) collective-permute-start(s32[4,16]{1,0:T(4,128)S(1)} %copy-done.2), channel_id=1, source_target_pairs={{0,1},{1,0},{2,3},{3,2},{4,5},{5,4},{6,7},{7,6},{8,9},{9,8},{10,11... | collective-permute-start | bytes 776 | tf_op jit(solution)/shard_map/ppermute | solution.py:484
  21.9 7.3 %collective-permute-start.4 = (f32[68,8,128]{2,1,0:T(8,128)S(1)}, f32[68,8,128]{2,1,0:T(8,128)S(1)}, u32[]{:S(2)}, u32[]{:S(2)}) collective-permute-start(f32[68,8,128]{2,1,0:T(8,128)S(1)} %get-tuple-element.18), channel_id=1, source_target_pairs={{0,128},{1,33},{2,130},{3,35},{4,132},{5,37},{6,134},{7,39},{8,136... | collective-permute-start | bytes 835592 | tf_op jit(solution)/shard_map/ppermute | solution.py:493
  22.0 10.0 %collective-permute-start.5 = (f32[68,8,128]{2,1,0:T(8,128)S(1)}, f32[68,8,128]{2,1,0:T(8,128)S(1)}, u32[]{:S(2)}, u32[]{:S(2)}) collective-permute-start(f32[68,8,128]{2,1,0:T(8,128)S(1)} %get-tuple-element.19), channel_id=1, source_target_pairs={{0,64},{1,17},{2,66},{3,19},{4,68},{5,21},{6,70},{7,23},{8,72},{9,... | collective-permute-start | bytes 835592 | tf_op jit(solution)/shard_map/ppermute | solution.py:493
  22.1 9.9 %collective-permute-start.6 = (f32[68,8,128]{2,1,0:T(8,128)S(1)}, f32[68,8,128]{2,1,0:T(8,128)S(1)}, u32[]{:S(2)}, u32[]{:S(2)}) collective-permute-start(f32[68,8,128]{2,1,0:T(8,128)S(1)} %get-tuple-element.20), channel_id=1, source_target_pairs={{0,192},{1,49},{2,194},{3,51},{4,196},{5,53},{6,198},{7,55},{8,200... | collective-permute-start | bytes 835592 | tf_op jit(solution)/shard_map/ppermute | solution.py:493
  32.1 3.2 %collective-permute-start.9 = (f32[17,8,128]{2,1,0:T(8,128)S(1)}, f32[17,8,128]{2,1,0:T(8,128)S(1)}, u32[]{:S(2)}, u32[]{:S(2)}) collective-permute-start(f32[17,8,128]{2,1,0:T(8,128)S(1)} %get-tuple-element.21), channel_id=1, source_target_pairs={{0,48},{1,193},{2,50},{3,195},{4,52},{5,197},{6,54},{7,199},{8,56}... | collective-permute-start | bytes 208904 | tf_op jit(solution)/shard_map/ppermute | solution.py:497
  32.7 4.4 %collective-permute-start.8 = (f32[17,8,128]{2,1,0:T(8,128)S(1)}, f32[17,8,128]{2,1,0:T(8,128)S(1)}, u32[]{:S(2)}, u32[]{:S(2)}) collective-permute-start(f32[17,8,128]{2,1,0:T(8,128)S(1)} %get-tuple-element.22), channel_id=1, source_target_pairs={{0,16},{1,65},{2,18},{3,67},{4,20},{5,69},{6,22},{7,71},{8,24},{9,... | collective-permute-start | bytes 208904 | tf_op jit(solution)/shard_map/ppermute | solution.py:497
  33.6 4.7 %collective-permute-start.7 = (f32[17,8,128]{2,1,0:T(8,128)S(1)}, f32[17,8,128]{2,1,0:T(8,128)S(1)}, u32[]{:S(2)}, u32[]{:S(2)}) collective-permute-start(f32[17,8,128]{2,1,0:T(8,128)S(1)} %get-tuple-element.23), channel_id=1, source_target_pairs={{0,32},{1,129},{2,34},{3,131},{4,36},{5,133},{6,38},{7,135},{8,40}... | collective-permute-start | bytes 208904 | tf_op jit(solution)/shard_map/ppermute | solution.py:497
  50.6 5.0 %collective-permute-start.10 = (f32[24,128]{1,0:T(8,128)S(1)}, f32[24,128]{1,0:T(8,128)S(1)}, u32[]{:S(2)}, u32[]{:S(2)}) collective-permute-start(f32[24,128]{1,0:T(8,128)S(1)} %bitcast.2), channel_id=1, source_target_pairs={{0,1},{1,0},{2,3},{3,2},{4,5},{5,4},{6,7},{7,6},{8,9},{9,8},{10,11... | collective-permute-start | bytes 36872 | tf_op jit(solution)/shard_map/ppermute | solution.py:500
